TPU v7x, 256 devices: a whole 4x4x8 slice. The times are simulated.
256 devices in a mesh: die: 4 (over x), tile: 64 (over y, z, core).
Axes of the slice: x: 4, y: 4, z: 8, core: 2. Of those that a mesh axis runs over, the one named last changes fastest.
Arguments:
- source_heating: float32 [16, 1024, 2048], P('die', 'tile'), may hold values from -96 to 96, as said below
- material_thermal_values: float32 [6], replicated, may hold values from 0.5 to 8
- layer_material: int32 [16], P('die'), may hold values from 0 to 5
- via_conductance: float32 [4], P('die'), may hold values from 2 to 16
- via_blocks: int32 [4, 24, 4], P('die'), may hold values from 0 to 2048, as said below
Outputs:
- thermal_solution: float32 [16, 1024, 2048], P('die', 'tile')
- balance_defect: float32 [16, 1024, 2048], P('die', 'tile')
Inputs may be any that keep to these rules, and one draw needn't show every extreme that they name: `via_blocks`: entry (d, b) is (first row, first column, height, width) of via block b on top of die d, joining die d's top layer to die d + 1's bottom layer, or to the cooled lid for the top die. Height is 8, 16 or 32 and width 16, 32 or 64, each cut to the plane's 1024 x 2048 cells; every block lies inside the plane; blocks may intersect. `source_heating`: heat per cell.
All inputs are finite; a program needn't handle non-finite values.
Results may differ from a plain program's by a relative error of at most 0.0003.
Values sent between devices are 32-bit elements; how exact they have to be, the bound alone decides.
A program may use at most 128 MiB of HBM per device.

v0:
```python
import jax
import jax.numpy as jnp
from jax import lax
from jax.sharding import PartitionSpec as P

NU = 2
NC = 6


OMEGA = 0.8


def from_behind(value, axis, steps):
    count = lax.axis_size(axis)
    leading, last = (max(0, -steps), min(count, count - steps))
    return lax.ppermute(value, axis, [(source, source + steps) for source in range(leading, last)])


def extended(x, sides, width):
    edges = {}
    for axis, dim in sides:
        size, length = (lax.axis_size(axis), x.shape[dim])
        up = [(i, (i + 1) % size) for i in range(size - 1)]
        last = lax.slice_in_dim(x, length - width, length, axis=dim)
        leading = lax.slice_in_dim(x, 0, width, axis=dim)
        edges[dim] = (
            lax.ppermute(last, axis, up),
            lax.ppermute(leading, axis, [(b, a) for a, b in up]),
        )
    done = []
    for _, dim in sides:
        low, high = edges[dim]
        around = [(width, width) if d in done else (0, 0) for d in range(x.ndim)]
        x = jnp.concatenate([jnp.pad(low, around), x, jnp.pad(high, around)], axis=dim)
        done.append(dim)
    return x


def block_sums(field):
    depth, height, lateral_extent = field.shape
    return field.reshape(depth, height // 4, 4, lateral_extent // 4, 4).sum(axis=(2, 4))


def spread_out(field):
    return jnp.repeat(jnp.repeat(field, 4, axis=1), 4, axis=2)


def stencil(padded, field, stencil_coefficients, diagonal, upper, lower):
    side = (
        padded[1:-1, 2:, 1:-1]
        + padded[1:-1, :-2, 1:-1]
        + padded[1:-1, 1:-1, 2:]
        + padded[1:-1, 1:-1, :-2]
    )
    return (
        diagonal * field
        - stencil_coefficients[:, None, None] * side
        - upper * padded[2:, 1:-1, 1:-1]
        - lower * padded[:-2, 1:-1, 1:-1]
    )


def local(source_heating, material_thermal_values, layer_material, via_conductance, via_blocks):
    layer_list, rows, width = source_heating.shape
    tile_pos = lax.axis_index("tile")
    onehot = (
        layer_material[:, None]
        == jnp.arange(material_thermal_values.shape[0], dtype=jnp.int32)[None, :]
    ).astype(jnp.float32)
    layer_cond = jnp.sum(onehot * material_thermal_values[None, :], axis=1)
    following = jnp.concatenate([layer_cond[1:], layer_cond[-1:]])
    vertical = 2.0 * layer_cond * following / (layer_cond + following)
    row_ids = tile_pos * rows + jnp.arange(rows, dtype=jnp.int32)
    col_ids = jnp.arange(width, dtype=jnp.int32)
    blocks = via_blocks[0]
    input_rows = (
        (row_ids[None, :] >= blocks[:, 0:1]) & (row_ids[None, :] < blocks[:, 0:1] + blocks[:, 2:3])
    ).astype(jnp.float32)
    in_cols = (
        (col_ids[None, :] >= blocks[:, 1:2]) & (col_ids[None, :] < blocks[:, 1:2] + blocks[:, 3:4])
    ).astype(jnp.float32)
    via_plane = (
        jnp.dot(
            input_rows.T,
            in_cols,
            precision=lax.Precision.HIGHEST,
            preferred_element_type=jnp.float32,
        )
        * via_conductance[0]
    )
    placed_above = jnp.arange(layer_list, dtype=jnp.int32) == layer_list - 1
    upper_zero = jnp.where(placed_above[:, None, None], via_plane[None], vertical[:, None, None])
    below = from_behind(via_plane, "die", 1)
    lower_zero = jnp.concatenate([below[None], upper_zero[:-1]], axis=0)
    upper_one = block_sums(upper_zero)
    lower_one = block_sums(lower_zero)
    uppers = [upper_zero, upper_one, block_sums(upper_one)]
    lowers = [lower_zero, lower_one, block_sums(lower_one)]
    stencil_coefficients = [layer_cond, layer_cond * 4.0, layer_cond * 16.0]
    diagonals = [
        4.0 * stencil_coefficients[lev][:, None, None] + uppers[lev] + lowers[lev]
        for lev in range(3)
    ]

    def conduction_product(field, level):
        if level == 0:
            padded = extended(field, (("die", 0), ("tile", 1)), 1)
        elif level == 1:
            padded = extended(field, (("die", 0), ("tile", 1)), 1)
        else:
            padded = extended(field, (("die", 0), ("tile", 1)), 1)
        padded = jnp.pad(padded, ((0, 0), (0, 0), (1, 1)))
        return stencil(
            padded,
            field,
            stencil_coefficients[level],
            diagonals[level],
            uppers[level],
            lowers[level],
        )

    def coarse_solve(rhs):
        field = OMEGA * rhs / diagonals[2]
        for sweep_index in range(NC - 1):
            field = field + OMEGA * (rhs - conduction_product(field, 2)) / diagonals[2]
        return field

    def smooth(field, rhs, level):
        return field + OMEGA * (rhs - conduction_product(field, level)) / diagonals[level]

    def hierarchy_round(level, rhs, field):
        if level == 2:
            return coarse_solve(rhs)
        sweeps = NU
        if field is None:
            field = OMEGA * rhs / diagonals[level]
            sweeps = sweeps - 1
        for sweep_index in range(sweeps):
            field = smooth(field, rhs, level)
        remainder = rhs - conduction_product(field, level)
        field = field + spread_out(hierarchy_round(level + 1, block_sums(remainder), None))
        for sweep_index in range(NU):
            field = smooth(field, rhs, level)
        return field

    thermal_solution = hierarchy_round(0, source_heating, None)
    thermal_solution = hierarchy_round(0, source_heating, thermal_solution)
    balance_defect = source_heating - conduction_product(thermal_solution, 0)
    return (thermal_solution, balance_defect)


def solution(mesh):
    in_specs = (P("die", "tile", None), P(), P("die"), P("die"), P("die", None, None))
    out_specs = (P("die", "tile", None), P("die", "tile", None))
    return jax.shard_map(local, mesh=mesh, in_specs=in_specs, out_specs=out_specs, check_vma=False)
```

profile of v0, /device:TPU:26, one launch (start us, length us, event | category | flops | bytes accessed | tf_op | source)
XLA Modules:
  0.0 556.3 jit_solution(14670791981249039131)
XLA Ops:
  7.3 5.6 %broadcast_in_dim.59 = f32[4,4,512,4]{3,2,1,0:T(8,128)} reshape(f32[16,2048]{1,0:T(8,128)S(1)} %convolution_multiply_fusion) | data formatting | bytes 262144 | tf_op jit(solution)/shard_map/jit(_where)/broadcast_in_dim | solution.py:92
  13.9 14.3 %concatenate.479 = f32[3,4,4,512,4]{4,3,2,1,0:T(8,128)} reshape(f32[3,16,2048]{2,1,0:T(8,128)S(1)} %slice.1290) | data formatting | bytes 786432 | tf_op jit(solution)/shard_map/concatenate | solution.py:94
  37.6 6.5 %collective-permute-start.3 = (f32[4,1,2048]{2,0,1:T(4,128)S(1)}, f32[4,1,2048]{2,0,1:T(4,128)S(1)}, u32[]{:S(2)}, u32[]{:S(2)}) collective-permute-start(f32[4,1,2048]{2,0,1:T(4,128)S(1)} %copy.388), channel_id=1, source_target_pairs={{1,0},{2,1},{3,2},{4,3},{5,4},{6,5},{7,6},{8,7},{9,8},{10,9},{11,1... | collective-permute-start | bytes 98312 | tf_op jit(solution)/shard_map/ppermute | solution.py:28
  46.1 5.7 %concatenate.478 = f32[1,4,4,512,4]{4,3,2,1,0:T(8,128)} reshape(f32[16,2048]{1,0:T(8,128)S(1)} %collective-permute-done) | data formatting | bytes 262144 | tf_op jit(solution)/shard_map/concatenate | solution.py:94
  51.8 4.6 constant_dynamic-update-slice_fusion.1
  56.4 10.6 %constant_dynamic-update-slice_fusion = f32[4,4,4,512,4]{4,3,2,1,0:T(8,128)} fusion(f32[4,4,4,512,4]{4,3,2,1,0:T(8,128)} %constant_dynamic-update-slice_fusion.1, f32[3,4,4,512,4]{4,3,2,1,0:T(8,128)} %concatenate.479), kind=kLoop, calls=%fused_computation.514 | loop fusion | bytes 25165824 | tf_op jit(solution)/shard_map/concatenate | solution.py:94
  74.3 5.2 collective-permute-start.7
  81.7 8.2 %fusion.279 = (f32[4,512]{1,0:T(4,128)S(1)}, f32[4,4,512]{2,1,0:T(4,128)S(1)}) fusion(f32[4,4,4,512,4]{4,3,2,1,0:T(8,128)} %constant_dynamic-update-slice_fusion), kind=kLoop, calls=%fused_computation.663 | loop fusion | flops 251904 | bytes 565248 | tf_op jit(solution)/shard_map/reduce_sum | solution.py:41
  91.2 18.7 %reshape.283 = f32[4,4,4,512,4]{4,3,2,1,0:T(8,128)} reshape(f32[4,16,2048]{2,1,0:T(8,128)S(1)} %fusion.10) | data formatting | bytes 1048576 | tf_op jit(solution)/shard_map/reshape | solution.py:41
  109.9 7.0 %reduce_sum.97 = f32[4,4,512]{2,1,0:T(4,128)S(1)} reduce(f32[4,4,4,512,4]{4,3,2,1,0:T(8,128)} %reshape.283, f32[]{:T(128)} %constant.10.clone.1), dimensions={2,4}, to_apply=%region_1.2 | reduce | flops 122880 | bytes 557060 | tf_op jit(solution)/shard_map/reduce_sum | solution.py:41
  117.0 5.8 %collective-permute-start.11 = (f32[4,1,512]{2,1,0:T(1,128)S(1)}, f32[4,1,512]{2,1,0:T(1,128)S(1)}, u32[]{:S(2)}, u32[]{:S(2)}) collective-permute-start(f32[4,1,512]{2,1,0:T(1,128)S(1)} %get-tuple-element.83), channel_id=1, source_target_pairs={{1,0},{2,1},{3,2},{4,3},{5,4},{6,5},{7,6},{8,7},{9,8},{10,9},{11,1... | collective-permute-start | bytes 24584 | tf_op jit(solution)/shard_map/ppermute | solution.py:28
  160.1 5.0 collective-permute-done.18
  175.5 4.6 collective-permute-done.22
  190.4 4.6 collective-permute-done.26
  269.2 5.3 collective-permute-done.48
  286.3 4.8 collective-permute-done.52
  302.8 4.8 collective-permute-done.56
  319.4 4.8 collective-permute-done.60
  336.2 4.6 collective-permute-done.64
  342.0 18.7 %reshape.286 = f32[4,4,4,512,4]{4,3,2,1,0:T(8,128)} reshape(f32[4,16,2048]{2,1,0:T(8,128)S(1)} %fusion.37) | data formatting | bytes 1048576 | tf_op jit(solution)/shard_map/reshape | solution.py:41
  360.7 7.0 %reduce_sum.133 = f32[4,4,512]{2,1,0:T(4,128)S(1)} reduce(f32[4,4,4,512,4]{4,3,2,1,0:T(8,128)} %reshape.286, f32[]{:T(128)} %constant.10.clone.1), dimensions={2,4}, to_apply=%region_10.11 | reduce | flops 122880 | bytes 557060 | tf_op jit(solution)/shard_map/reduce_sum | solution.py:41
  406.1 5.0 collective-permute-done.74
  515.3 5.3 collective-permute-done.104
  548.9 4.8 collective-permute-done.112
  (447 shorter events, 379.9 us)
Async XLA Ops:
  2.4 29.0 %collective-permute-start = (f32[16,2048]{1,0:T(8,128)S(1)}, f32[16,2048]{1,0:T(8,128)S(1)}, u32[]{:S(2)}, u32[]{:S(2)}) collective-permute-start(f32[16,2048]{1,0:T(8,128)S(1)} %convolution_multiply_fusion), channel_id=1, source_target_pairs={{0,64},{64,128},{128,192},{1,65},{65,129},{129,193},{2,66},{66,130... | collective-permute-start | bytes 393224 | tf_op jit(solution)/shard_map/ppermute | solution.py:16
  31.7 35.5 %collective-permute-start.1 = (f32[1,16,2048]{2,1,0:T(8,128)S(1)}, f32[1,16,2048]{2,1,0:T(8,128)S(1)}, u32[]{:S(2)}, u32[]{:S(2)}) collective-permute-start(f32[1,16,2048]{2,1,0:T(8,128)S(1)} %get-tuple-element.53), channel_id=1, source_target_pairs={{0,64},{64,128},{128,192},{1,65},{65,129},{129,193},{2,66},{66,130... | collective-permute-start | bytes 393224 | tf_op jit(solution)/shard_map/ppermute | solution.py:27
  34.8 32.4 %collective-permute-start.2 = (f32[1,16,2048]{2,1,0:T(8,128)S(1)}, f32[1,16,2048]{2,1,0:T(8,128)S(1)}, u32[]{:S(2)}, u32[]{:S(2)}) collective-permute-start(f32[1,16,2048]{2,1,0:T(8,128)S(1)} %get-tuple-element.52), channel_id=1, source_target_pairs={{64,0},{128,64},{192,128},{65,1},{129,65},{193,129},{66,2},{130,66... | collective-permute-start | bytes 393224 | tf_op jit(solution)/shard_map/ppermute | solution.py:28
  37.6 29.4 %collective-permute-start.3 = (f32[4,1,2048]{2,0,1:T(4,128)S(1)}, f32[4,1,2048]{2,0,1:T(4,128)S(1)}, u32[]{:S(2)}, u32[]{:S(2)}) collective-permute-start(f32[4,1,2048]{2,0,1:T(4,128)S(1)} %copy.388), channel_id=1, source_target_pairs={{1,0},{2,1},{3,2},{4,3},{5,4},{6,5},{7,6},{8,7},{9,8},{10,9},{11,1... | collective-permute-start | bytes 98312 | tf_op jit(solution)/shard_map/ppermute | solution.py:28
  44.1 22.9 %collective-permute-start.4 = (f32[4,1,2048]{2,0,1:T(4,128)S(1)}, f32[4,1,2048]{2,0,1:T(4,128)S(1)}, u32[]{:S(2)}, u32[]{:S(2)}) collective-permute-start(f32[4,1,2048]{2,0,1:T(4,128)S(1)} %copy.390), channel_id=1, source_target_pairs={{0,1},{1,2},{2,3},{3,4},{4,5},{5,6},{6,7},{7,8},{8,9},{9,10},{10,1... | collective-permute-start | bytes 98312 | tf_op jit(solution)/shard_map/ppermute | solution.py:27
  68.5 21.6 %collective-permute-start.5 = (f32[1,16,2048]{2,1,0:T(8,128)S(1)}, f32[1,16,2048]{2,1,0:T(8,128)S(1)}, u32[]{:S(2)}, u32[]{:S(2)}) collective-permute-start(f32[1,16,2048]{2,1,0:T(8,128)S(1)} %get-tuple-element.49), channel_id=1, source_target_pairs={{0,64},{64,128},{128,192},{1,65},{65,129},{129,193},{2,66},{66,130... | collective-permute-start | bytes 393224 | tf_op jit(solution)/shard_map/ppermute | solution.py:27
  71.6 18.5 %collective-permute-start.6 = (f32[1,16,2048]{2,1,0:T(8,128)S(1)}, f32[1,16,2048]{2,1,0:T(8,128)S(1)}, u32[]{:S(2)}, u32[]{:S(2)}) collective-permute-start(f32[1,16,2048]{2,1,0:T(8,128)S(1)} %get-tuple-element.48), channel_id=1, source_target_pairs={{64,0},{128,64},{192,128},{65,1},{129,65},{193,129},{66,2},{130,66... | collective-permute-start | bytes 393224 | tf_op jit(solution)/shard_map/ppermute | solution.py:28
  74.3 15.5 %collective-permute-start.7 = (f32[4,1,2048]{2,0,1:T(4,128)S(1)}, f32[4,1,2048]{2,0,1:T(4,128)S(1)}, u32[]{:S(2)}, u32[]{:S(2)}) collective-permute-start(f32[4,1,2048]{2,0,1:T(4,128)S(1)} %copy.392), channel_id=1, source_target_pairs={{1,0},{2,1},{3,2},{4,3},{5,4},{6,5},{7,6},{8,7},{9,8},{10,9},{11,1... | collective-permute-start | bytes 98312 | tf_op jit(solution)/shard_map/ppermute | solution.py:28
  117.0 13.5 %collective-permute-start.11 = (f32[4,1,512]{2,1,0:T(1,128)S(1)}, f32[4,1,512]{2,1,0:T(1,128)S(1)}, u32[]{:S(2)}, u32[]{:S(2)}) collective-permute-start(f32[4,1,512]{2,1,0:T(1,128)S(1)} %get-tuple-element.83), channel_id=1, source_target_pairs={{1,0},{2,1},{3,2},{4,3},{5,4},{6,5},{7,6},{8,7},{9,8},{10,9},{11,1... | collective-permute-start | bytes 24584 | tf_op jit(solution)/shard_map/ppermute | solution.py:28
  257.5 17.2 %collective-permute-start.45 = (f32[1,16,2048]{2,1,0:T(8,128)S(1)}, f32[1,16,2048]{2,1,0:T(8,128)S(1)}, u32[]{:S(2)}, u32[]{:S(2)}) collective-permute-start(f32[1,16,2048]{2,1,0:T(8,128)S(1)} %get-tuple-element.45), channel_id=1, source_target_pairs={{0,64},{64,128},{128,192},{1,65},{65,129},{129,193},{2,66},{66,130... | collective-permute-start | bytes 393224 | tf_op jit(solution)/shard_map/ppermute | solution.py:27
  259.4 15.2 %collective-permute-start.46 = (f32[1,16,2048]{2,1,0:T(8,128)S(1)}, f32[1,16,2048]{2,1,0:T(8,128)S(1)}, u32[]{:S(2)}, u32[]{:S(2)}) collective-permute-start(f32[1,16,2048]{2,1,0:T(8,128)S(1)} %get-tuple-element.44), channel_id=1, source_target_pairs={{64,0},{128,64},{192,128},{65,1},{129,65},{193,129},{66,2},{130,66... | collective-permute-start | bytes 393224 | tf_op jit(solution)/shard_map/ppermute | solution.py:28
  275.9 15.3 %collective-permute-start.49 = (f32[1,16,2048]{2,1,0:T(8,128)S(1)}, f32[1,16,2048]{2,1,0:T(8,128)S(1)}, u32[]{:S(2)}, u32[]{:S(2)}) collective-permute-start(f32[1,16,2048]{2,1,0:T(8,128)S(1)} %get-tuple-element.41), channel_id=1, source_target_pairs={{0,64},{64,128},{128,192},{1,65},{65,129},{129,193},{2,66},{66,130... | collective-permute-start | bytes 393224 | tf_op jit(solution)/shard_map/ppermute | solution.py:27
  278.1 13.1 %collective-permute-start.50 = (f32[1,16,2048]{2,1,0:T(8,128)S(1)}, f32[1,16,2048]{2,1,0:T(8,128)S(1)}, u32[]{:S(2)}, u32[]{:S(2)}) collective-permute-start(f32[1,16,2048]{2,1,0:T(8,128)S(1)} %get-tuple-element.40), channel_id=1, source_target_pairs={{64,0},{128,64},{192,128},{65,1},{129,65},{193,129},{66,2},{130,66... | collective-permute-start | bytes 393224 | tf_op jit(solution)/shard_map/ppermute | solution.py:28
  292.4 15.3 %collective-permute-start.53 = (f32[1,16,2048]{2,1,0:T(8,128)S(1)}, f32[1,16,2048]{2,1,0:T(8,128)S(1)}, u32[]{:S(2)}, u32[]{:S(2)}) collective-permute-start(f32[1,16,2048]{2,1,0:T(8,128)S(1)} %get-tuple-element.37), channel_id=1, source_target_pairs={{0,64},{64,128},{128,192},{1,65},{65,129},{129,193},{2,66},{66,130... | collective-permute-start | bytes 393224 | tf_op jit(solution)/shard_map/ppermute | solution.py:27
  294.6 13.1 %collective-permute-start.54 = (f32[1,16,2048]{2,1,0:T(8,128)S(1)}, f32[1,16,2048]{2,1,0:T(8,128)S(1)}, u32[]{:S(2)}, u32[]{:S(2)}) collective-permute-start(f32[1,16,2048]{2,1,0:T(8,128)S(1)} %get-tuple-element.36), channel_id=1, source_target_pairs={{64,0},{128,64},{192,128},{65,1},{129,65},{193,129},{66,2},{130,66... | collective-permute-start | bytes 393224 | tf_op jit(solution)/shard_map/ppermute | solution.py:28
  309.0 15.3 %collective-permute-start.57 = (f32[1,16,2048]{2,1,0:T(8,128)S(1)}, f32[1,16,2048]{2,1,0:T(8,128)S(1)}, u32[]{:S(2)}, u32[]{:S(2)}) collective-permute-start(f32[1,16,2048]{2,1,0:T(8,128)S(1)} %get-tuple-element.33), channel_id=1, source_target_pairs={{0,64},{64,128},{128,192},{1,65},{65,129},{129,193},{2,66},{66,130... | collective-permute-start | bytes 393224 | tf_op jit(solution)/shard_map/ppermute | solution.py:27
  311.2 13.1 %collective-permute-start.58 = (f32[1,16,2048]{2,1,0:T(8,128)S(1)}, f32[1,16,2048]{2,1,0:T(8,128)S(1)}, u32[]{:S(2)}, u32[]{:S(2)}) collective-permute-start(f32[1,16,2048]{2,1,0:T(8,128)S(1)} %get-tuple-element.32), channel_id=1, source_target_pairs={{64,0},{128,64},{192,128},{65,1},{129,65},{193,129},{66,2},{130,66... | collective-permute-start | bytes 393224 | tf_op jit(solution)/shard_map/ppermute | solution.py:28
  325.5 15.3 %collective-permute-start.61 = (f32[1,16,2048]{2,1,0:T(8,128)S(1)}, f32[1,16,2048]{2,1,0:T(8,128)S(1)}, u32[]{:S(2)}, u32[]{:S(2)}) collective-permute-start(f32[1,16,2048]{2,1,0:T(8,128)S(1)} %get-tuple-element.29), channel_id=1, source_target_pairs={{0,64},{64,128},{128,192},{1,65},{65,129},{129,193},{2,66},{66,130... | collective-permute-start | bytes 393224 | tf_op jit(solution)/shard_map/ppermute | solution.py:27
  327.7 13.1 %collective-permute-start.62 = (f32[1,16,2048]{2,1,0:T(8,128)S(1)}, f32[1,16,2048]{2,1,0:T(8,128)S(1)}, u32[]{:S(2)}, u32[]{:S(2)}) collective-permute-start(f32[1,16,2048]{2,1,0:T(8,128)S(1)} %get-tuple-element.28), channel_id=1, source_target_pairs={{64,0},{128,64},{192,128},{65,1},{129,65},{193,129},{66,2},{130,66... | collective-permute-start | bytes 393224 | tf_op jit(solution)/shard_map/ppermute | solution.py:28
  503.5 17.2 %collective-permute-start.101 = (f32[1,16,2048]{2,1,0:T(8,128)S(1)}, f32[1,16,2048]{2,1,0:T(8,128)S(1)}, u32[]{:S(2)}, u32[]{:S(2)}) collective-permute-start(f32[1,16,2048]{2,1,0:T(8,128)S(1)} %get-tuple-element.25), channel_id=1, source_target_pairs={{0,64},{64,128},{128,192},{1,65},{65,129},{129,193},{2,66},{66,130... | collective-permute-start | bytes 393224 | tf_op jit(solution)/shard_map/ppermute | solution.py:27
  505.5 15.2 %collective-permute-start.102 = (f32[1,16,2048]{2,1,0:T(8,128)S(1)}, f32[1,16,2048]{2,1,0:T(8,128)S(1)}, u32[]{:S(2)}, u32[]{:S(2)}) collective-permute-start(f32[1,16,2048]{2,1,0:T(8,128)S(1)} %get-tuple-element.24), channel_id=1, source_target_pairs={{64,0},{128,64},{192,128},{65,1},{129,65},{193,129},{66,2},{130,66... | collective-permute-start | bytes 393224 | tf_op jit(solution)/shard_map/ppermute | solution.py:28
  521.9 15.3 %collective-permute-start.105 = (f32[1,16,2048]{2,1,0:T(8,128)S(1)}, f32[1,16,2048]{2,1,0:T(8,128)S(1)}, u32[]{:S(2)}, u32[]{:S(2)}) collective-permute-start(f32[1,16,2048]{2,1,0:T(8,128)S(1)} %get-tuple-element.21), channel_id=1, source_target_pairs={{0,64},{64,128},{128,192},{1,65},{65,129},{129,193},{2,66},{66,130... | collective-permute-start | bytes 393224 | tf_op jit(solution)/shard_map/ppermute | solution.py:27
  538.5 15.3 %collective-permute-start.109 = (f32[1,16,2048]{2,1,0:T(8,128)S(1)}, f32[1,16,2048]{2,1,0:T(8,128)S(1)}, u32[]{:S(2)}, u32[]{:S(2)}) collective-permute-start(f32[1,16,2048]{2,1,0:T(8,128)S(1)} %get-tuple-element.17), channel_id=1, source_target_pairs={{0,64},{64,128},{128,192},{1,65},{65,129},{129,193},{2,66},{66,130... | collective-permute-start | bytes 393224 | tf_op jit(solution)/shard_map/ppermute | solution.py:27
  540.7 13.1 %collective-permute-start.110 = (f32[1,16,2048]{2,1,0:T(8,128)S(1)}, f32[1,16,2048]{2,1,0:T(8,128)S(1)}, u32[]{:S(2)}, u32[]{:S(2)}) collective-permute-start(f32[1,16,2048]{2,1,0:T(8,128)S(1)} %get-tuple-element.16), channel_id=1, source_target_pairs={{64,0},{128,64},{192,128},{65,1},{129,65},{193,129},{66,2},{130,66... | collective-permute-start | bytes 393224 | tf_op jit(solution)/shard_map/ppermute | solution.py:28
  (91 other events, 666.1 us)
where the time goes:
time: 566 us; the launch traced here: 556 us
  starting transfers between devices  311 us (55%)
  waiting for transfers between devices  100 us (18%)
  local copies, waits for them, and re-layouts  98 us (17%)
  other arithmetic  42 us (7%)
    ppermute x56, starting transfers between devices, extended(): lax.ppermute(leading, axis, [(b, a) for a, b in up])  181 us
    ppermute x56, starting transfers between devices, extended(): lax.ppermute(last, axis, up)  127 us
    ppermute x56, waiting for transfers between devices, extended(): lax.ppermute(last, axis, up)  85.7 us
    reshape x2, local copies, waits for them, and re-layouts, block_sums(): field.reshape(depth, height // 4, 4, lateral_extent // 4, 4)  37.4 us
    concatenate x3, local copies, waits for them, and re-layouts, local(): lower_zero = jnp.concatenate([below[None], upper_zero[:-1]], axis=0)  30.6 us
    reduce_sum x10, other arithmetic, block_sums(): field.reshape(depth, height // 4, 4, lateral_extent // 4, 4)  23.3 us
    ppermute x56, waiting for transfers between devices, extended(): lax.ppermute(leading, axis, [(b, a) for a, b in up])  14.5 us
  transfers between devices with their start and end apart: 113, of which 26 were waited for; matrix products, arithmetic and copies ran while one was open for 10% of the time, Pallas kernels for 0%

commit v1 on v0

v1 whole, which is shorter than its diff:
```python
import functools

import jax
import jax.numpy as jnp
from jax import lax
from jax.experimental import pallas as pl
from jax.experimental.pallas import tpu as pltpu
from jax.sharding import PartitionSpec as P

F32 = jnp.float32
OMEGA = 0.8
KEEP = 1.0 - OMEGA
LZ = 4
ROWS = 16
HY = 6
NYW = ROWS + 2 * HY
NW = 3 * LZ
K = 16
LANES = 128
H1 = 5
N1 = 4 + 2 * H1
H2 = 6
N2 = 1 + 2 * H2
NZ = 16


def rows_of(y, count=1):
    start = y * K
    if not isinstance(start, int):
        start = pl.multiple_of(start, K)
    return pl.ds(start, count * K)


def kernel(n_tile, f_in, pk, v_out, b_out, f, v0, v1, v2, vn, vd_top, wlo, whi, pall, cz,
           turn, restr, r1g, r1, w1, u1, l1, a1, b1, r2, w2, u2, l2, a2, b2, via1, send_sem, recv_sem):
    d = lax.axis_index("die")
    t = lax.axis_index("tile")

    def at(dd, dt):
        return {"die": lax.rem(d + dd + 4, 4), "tile": lax.rem(t + dt + n_tile, n_tile)}

    counter = [0]

    def push(src, dst, dd, dt):
        i = counter[0]
        counter[0] += 1
        copy = pltpu.make_async_remote_copy(
            src_ref=src, dst_ref=dst, send_sem=send_sem.at[i], recv_sem=recv_sem.at[i],
            device_id=at(dd, dt), device_id_type=pl.DeviceIdType.MESH)
        copy.start()
        return copy

    def arrived(copies):
        for copy in copies:
            copy.wait_recv()

    def sent(copies):
        for copy in copies:
            copy.wait_send()

    partners = [(1, 0), (2, 0), (3, 0), (1, 1), (1, -1), (-1, 1), (-1, -1)]
    partners += [(0, s * j) for j in range(1, H2 + 1) for s in (1, -1)]
    barrier = pltpu.get_barrier_semaphore()
    for dd, dt in partners:
        pl.semaphore_signal(barrier, inc=1, device_id=at(dd, dt), device_id_type=pl.DeviceIdType.MESH)

    for m in range(K):
        block = f_in[:, :, m * LANES:(m + 1) * LANES].reshape(LZ * ROWS, LANES)
        turn[m * LANES:(m + 1) * LANES, 0:LZ * ROWS] = block.T
    for k in range(K):
        block = turn[pl.ds(k, LANES, stride=K), 0:LZ * ROWS].T
        for z in range(LZ):
            f[LZ + z, pl.ds(HY * K + k, ROWS, stride=K), :] = block[z * ROWS:(z + 1) * ROWS]
    zero_row = jnp.zeros((K, LANES), F32)

    def clear(y, carry):
        for w in range(NW):
            v2[w, rows_of(y), :] = zero_row
        v1[0, rows_of(y), :] = zero_row
        v1[NW - 1, rows_of(y), :] = zero_row
        return carry

    lax.fori_loop(0, NYW, clear, 0)
    pall[d] = pk[...]

    pl.semaphore_wait(barrier, len(partners))

    own = rows_of(HY, ROWS)
    last = HY + ROWS - 1
    par = [push(pk, pall.at[d], dd, 0) for dd in (1, 2, 3)]
    near = [
        push(f.at[7, own], f.at[3, own], 1, 0),
        push(f.at[4, own], f.at[8, own], -1, 0),
        push(f.at[pl.ds(4, 4), rows_of(last + 1 - HY, HY)], f.at[pl.ds(4, 4), rows_of(0, HY)], 0, 1),
        push(f.at[pl.ds(4, 4), rows_of(HY, HY)], f.at[pl.ds(4, 4), rows_of(HY + ROWS, HY)], 0, -1),
        push(f.at[7, rows_of(last)], f.at[3, rows_of(HY - 1)], 1, 1),
        push(f.at[7, rows_of(HY)], f.at[3, rows_of(last + 1)], 1, -1),
        push(f.at[4, rows_of(last)], f.at[8, rows_of(HY - 1)], -1, 1),
        push(f.at[4, rows_of(HY)], f.at[8, rows_of(last + 1)], -1, -1),
    ]
    bulk = [
        push(f.at[pl.ds(5, 2), own], f.at[pl.ds(1, 2), own], 1, 0),
        push(f.at[pl.ds(5, 2), own], f.at[pl.ds(9, 2), own], -1, 0),
    ]

    arrived(par)

    def coverage(e, rows, row0, cell, lanes_cols):
        n_lanes = lanes_cols * LANES
        prm = pall[e]
        lane = lax.broadcasted_iota(jnp.int32, (24, n_lanes), 1)
        col = (((lane & (LANES - 1)) * lanes_cols + (lane >> 7)) * cell).astype(F32)
        c_lo, c_hi = prm[0:24, 1:2], prm[0:24, 1:2] + prm[0:24, 3:4]
        cols = jnp.maximum(jnp.minimum(c_hi, col + cell) - jnp.maximum(c_lo, col), 0.0)
        row = ((row0 + lax.broadcasted_iota(jnp.int32, (rows, LANES), 0)) * cell).astype(F32)
        r_lo, r_hi = prm[29:30, :], prm[29:30, :] + prm[30:31, :]
        cover = jnp.maximum(jnp.minimum(r_hi, row + cell) - jnp.maximum(r_lo, row), 0.0)
        return jnp.dot(cover[:, 0:24], cols, precision=lax.Precision.HIGHEST,
                       preferred_element_type=F32) * prm[28:29, 0:1]

    cond = jnp.concatenate([pall[e, 24:28, :] for e in range(4)], axis=0)
    follow = jnp.concatenate([cond[1:], cond[NZ - 1:]], axis=0)
    vert = 2.0 * cond * follow / (cond + follow)
    cz[0] = cond
    cz[1] = vert

    zs = lax.broadcasted_iota(jnp.int32, (NZ, LANES), 0)
    is_top = (zs & 3) == 3
    is_end = zs == NZ - 1
    lanes8 = lax.broadcasted_iota(jnp.int32, (8, LANES), 1)
    subs8 = lax.broadcasted_iota(jnp.int32, (8, LANES), 0)
    lanes16 = lax.broadcasted_iota(jnp.int32, (NZ, LANES), 1)

    def valid(row, count):
        return jnp.where((row >= 0) & (row < count), 1.0, 0.0).astype(F32)

    def fine_valid(y):
        return valid(t * ROWS - HY + y, n_tile * ROWS)

    for j in range(4):
        e = lax.rem(d + 2 + j, 4)
        plane = coverage(e, 32, t * ROWS - HY, 1, K)
        for k in range(K):
            vn[j, pl.ds(k, NYW, stride=K), :] = plane[0:NYW, k * LANES:(k + 1) * LANES]

    def zrow(which, w):
        z = lax.rem(LZ * (d + 3) + w, NZ)
        return cz[which, pl.ds(z, 1), :]

    def splat(w):
        ty = w % LZ
        c = zrow(0, w)
        u = zrow(1, w) if ty < 3 else None
        lo = zrow(1, w - 1) if ty > 0 else None
        return c, u, lo

    edge = [jnp.where(lax.rem(d + 2 + j, 4) == 3, 0.0, 1.0).astype(F32) for j in range(4)]
    ends = [(splat(LZ * m), splat(LZ * m + 3)) for m in range(3)]

    def fine_weights(y, carry):
        ok = fine_valid(y) * OMEGA
        planes = [vn[j, rows_of(y), :] for j in range(4)]
        coupled = [planes[j] * edge[j] for j in range(4)]
        vd_top[rows_of(y), :] = planes[2]
        for j in range(4):
            vn[j, rows_of(y), :] = coupled[j]
        for m in range(3):
            (c, u, _), (ct, _, lt) = ends[m]
            wlo[m, rows_of(y), :] = ok / (4.0 * c + u + coupled[m])
            whi[m, rows_of(y), :] = ok / (4.0 * ct + lt + planes[m + 1])
        return carry

    lax.fori_loop(0, NYW, fine_weights, 0)

    def coarse_coeffs(via_rows, scale, couple, row_ok):
        via = jnp.zeros((NZ, LANES), F32)
        for e in range(4):
            via = jnp.where(zs == LZ * e + 3, via_rows[e], via)
        upper = jnp.where(is_top, via, vert * couple)
        nb = jnp.where(is_end, 0.0, upper)
        lower = pltpu.roll(nb, 1, 0)
        return (row_ok * OMEGA) / (4.0 * scale * cond + upper + lower), nb, lower

    for e in range(4):
        plane = coverage(e, 16, t * 4 - H1, 4, 4)
        for p in range(4):
            via1[e, p * 16:(p + 1) * 16, :] = plane[:, p * LANES:(p + 1) * LANES]
        via1[e, 64:80, :] = coverage(e, 16, t - H2, 16, 1)

    def mid_coeffs(i, carry):
        ok = valid(t * 4 - H1 + i, n_tile * 4)
        for p in range(4):
            got = coarse_coeffs([via1[e, pl.ds(p * 16 + i, 1), :] for e in range(4)], 4.0, 16.0, ok)
            w1[i * 4 + p], u1[i * 4 + p], l1[i * 4 + p] = got
        return carry

    lax.fori_loop(0, N1, mid_coeffs, 0)

    def low_coeffs(i, carry):
        ok = valid(t - H2 + i, n_tile)
        got = coarse_coeffs([via1[e, pl.ds(64 + i, 1), :] for e in range(4)], 16.0, 256.0, ok)
        w2[i], u2[i], l2[i] = got
        return carry

    lax.fori_loop(0, N2, low_coeffs, 0)

    def beside(x):
        nxt = pltpu.roll(x, K - 1, 0)
        prv = pltpu.roll(x, 1, 0)
        n_lo, n_hi = nxt[0:8], nxt[8:16]
        p_lo, p_hi = prv[0:8], prv[8:16]
        n_in = jnp.where(lanes8 == LANES - 1, 0.0, pltpu.roll(n_hi, LANES - 1, 1))
        p_in = jnp.where(lanes8 == 0, 0.0, pltpu.roll(p_lo, 1, 1))
        n_hi = jnp.where(subs8 == 7, n_in, n_hi)
        p_lo = jnp.where(subs8 == 0, p_in, p_lo)
        return jnp.concatenate([n_lo + p_lo, n_hi + p_hi], axis=0)

    def flows(src, w, y, consts, above=True, below=True):
        c, u, lo = consts
        ty, m = w % LZ, w // LZ
        x = src[w, rows_of(y), :]
        side = (src[w, rows_of(y - 1), :] + src[w, rows_of(y + 1), :]) + beside(x)
        total = f[w, rows_of(y), :] + c * side
        if above:
            total += (vn[m + 1, rows_of(y), :] if ty == 3 else u) * src[w + 1, rows_of(y), :]
        if below:
            total += (vn[m, rows_of(y), :] if ty == 0 else lo) * src[w - 1, rows_of(y), :]
        return x, total

    def plain_weight(consts):
        c, u, lo = consts
        return OMEGA / (4.0 * c + u + lo)

    def weight(w, y, plain):
        ty, m = w % LZ, w // LZ
        if ty == 0:
            return wlo[m, rows_of(y), :]
        if ty == 3:
            return whi[m, rows_of(y), :]
        return plain * fine_valid(y)

    def layer_consts(layers):
        consts = {w: splat(w) for w in layers}
        plain = {w: plain_weight(consts[w]) for w in layers if w % LZ in (1, 2)}
        return consts, plain

    def start_from_zero(dst, layers, y_lo, y_hi):
        _, plain = layer_consts(layers)

        def body(y, carry):
            for w in layers:
                dst[w, rows_of(y), :] = weight(w, y, plain.get(w)) * f[w, rows_of(y), :]
            return carry

        lax.fori_loop(y_lo, y_hi, body, 0)

    def sweep(src, dst, layers, y_lo, y_hi):
        consts, plain = layer_consts(layers)

        def body(y, carry):
            for w in layers:
                x, total = flows(src, w, y, consts[w])
                dst[w, rows_of(y), :] = KEEP * x + weight(w, y, plain.get(w)) * total
            return carry

        lax.fori_loop(y_lo, y_hi, body, 0)

    def diagonal(w, y, consts):
        c, u, lo = consts
        if w == LZ:
            return 4.0 * c + u + vn[1, rows_of(y), :]
        if w == LZ + 3:
            return 4.0 * c + lo + vd_top[rows_of(y), :]
        return 4.0 * c + u + lo

    own_layers = list(range(LZ, 2 * LZ))

    def restricted_residual(src, slot):
        consts, _ = layer_consts(own_layers)

        def body(i, carry):
            sums = [None] * 6
            for q in range(4):
                y = HY + i * 4 + q
                parts = []
                for w in own_layers:
                    x, total = flows(src, w, y, consts[w], above=w < LZ + 3, below=w > LZ)
                    parts.append(total - diagonal(w, y, consts[w]) * x)
                parts.append(vn[1, rows_of(y), :] * src[LZ, rows_of(y), :])
                parts.append(vn[2, rows_of(y), :] * src[LZ + 3, rows_of(y), :])
                sums = [p if s is None else s + p for s, p in zip(sums, parts)]
            for s in range(6):
                restr[pl.ds(pl.multiple_of((i * 8 + s) * K, K), K), :] = sums[s]
            for s in (6, 7):
                restr[pl.ds(pl.multiple_of((i * 8 + s) * K, K), K), :] = zero_row
            return carry

        lax.fori_loop(0, 4, body, 0)
        for i in range(4):
            for p in range(4):
                tile = restr[pl.ds(i * 128 + 4 * p, 8, stride=K), :]
                for q in range(1, 4):
                    tile += restr[pl.ds(i * 128 + 4 * p + q, 8, stride=K), :]
                r1g[slot, d, i * 4 + p] = tile

    mid_c = 4.0 * cond
    low_c = 16.0 * cond

    def lane_next(x):
        return jnp.where(lanes16 == LANES - 1, 0.0, pltpu.roll(x, LANES - 1, 1))

    def lane_prev(x):
        return jnp.where(lanes16 == 0, 0.0, pltpu.roll(x, 1, 1))

    def mid_flows(src, rhs, i):
        xs = [src[i * 4 + p] for p in range(4)]
        out = []
        for p in range(4):
            nxt = xs[p + 1] if p < 3 else lane_next(xs[0])
            prv = xs[p - 1] if p > 0 else lane_prev(xs[3])
            side = (src[i * 4 - 4 + p] + src[i * 4 + 4 + p]) + (nxt + prv)
            total = rhs[i * 4 + p] + mid_c * side
            total += u1[i * 4 + p] * pltpu.roll(xs[p], NZ - 1, 0)
            total += l1[i * 4 + p] * pltpu.roll(xs[p], 1, 0)
            out.append((xs[p], total))
        return out

    def mid_sweep(src, dst, rhs, lo, hi):
        def body(i, carry):
            for p, (x, total) in enumerate(mid_flows(src, rhs, i)):
                dst[i * 4 + p] = KEEP * x + w1[i * 4 + p] * total
            return carry

        lax.fori_loop(lo, hi, body, 0)

    def assemble(slot):
        def body(i, carry):
            for p in range(4):
                ts = [r1g[slot, e, i * 4 + p] for e in range(4)]

                def put(e, src_row, dst_row):
                    return jnp.where(subs8 == dst_row, pltpu.roll(ts[e], (dst_row - src_row) % 8, 0), 0.0)

                lo = jnp.where(subs8 < 4, ts[0], pltpu.roll(ts[1], 4, 0))
                lo += put(1, 4, 3) + put(0, 5, 4) + put(2, 4, 7)
                hi = jnp.where(subs8 < 4, ts[2], pltpu.roll(ts[3], 4, 0))
                hi += put(1, 5, 0) + put(3, 4, 3) + put(2, 5, 4)
                r1[slot, (H1 + i) * 4 + p] = jnp.concatenate([lo, hi], axis=0)
            return carry

        lax.fori_loop(0, 4, body, 0)

    def coarse_cycle(slot, after_gather, while_waiting):
        gather = [push(r1g.at[slot, d], r1g.at[slot, d], dd, 0) for dd in (1, 3, 2)]
        extra = after_gather()
        arrived(gather)
        assemble(slot)
        rhs = r1.at[slot]
        spread = [
            push(rhs.at[pl.ds(H1 * 4, 16)], rhs.at[pl.ds((H1 - 4) * 4, 16)], 0, 1),
            push(rhs.at[pl.ds(H1 * 4, 16)], rhs.at[pl.ds((H1 + 4) * 4, 16)], 0, -1),
            push(rhs.at[pl.ds((H1 + 3) * 4, 4)], rhs.at[pl.ds(0, 4)], 0, 2),
            push(rhs.at[pl.ds(H1 * 4, 4)], rhs.at[pl.ds((N1 - 1) * 4, 4)], 0, -2),
        ]
        arrived(spread)

        def first(i, carry):
            for p in range(4):
                a1[i * 4 + p] = w1[i * 4 + p] * rhs[i * 4 + p]
            return carry

        lax.fori_loop(0, N1, first, 0)
        mid_sweep(a1, b1, rhs, 1, N1 - 1)

        def down(i, acc):
            for p, (x, total) in enumerate(mid_flows(b1, rhs, i)):
                acc += total - (OMEGA / w1[i * 4 + p]) * x
            return acc

        r2[slot, H2] = lax.fori_loop(H1, H1 + 4, down, jnp.zeros((NZ, LANES), F32))
        low = []
        for j in range(1, H2 + 1):
            low.append(push(r2.at[slot, H2], r2.at[slot, H2 - j], 0, j))
            low.append(push(r2.at[slot, H2], r2.at[slot, H2 + j], 0, -j))
        extra = extra + while_waiting(extra)
        arrived(low)

        bufs = (a2, b2)
        for i in range(N2):
            a2[i] = w2[i] * r2[slot, i]
        for s in range(5):
            src, dst = bufs[s % 2], bufs[(s + 1) % 2]
            for i in range(s + 1, N2 - 1 - s):
                x = src[i]
                side = (src[i - 1] + src[i + 1]) + (lane_next(x) + lane_prev(x))
                total = r2[slot, i] + low_c * side
                total += u2[i] * pltpu.roll(x, NZ - 1, 0) + l2[i] * pltpu.roll(x, 1, 0)
                dst[i] = KEEP * x + w2[i] * total
        fix = bufs[1]
        for g in range(3):
            e2 = fix[H2 - 1 + g]
            for i in range(4):
                for p in range(4):
                    at_cell = (H1 - 4 + g * 4 + i) * 4 + p
                    b1[at_cell] = b1[at_cell] + e2
        mid_sweep(b1, a1, rhs, 2, N1 - 2)
        mid_sweep(a1, b1, rhs, 3, N1 - 3)
        sent(gather + spread + low)
        return extra

    def correction(i, w):
        z = lax.rem(LZ * (d + 3) + w, NZ)
        rows = [b1[i * 4 + p, pl.ds(z, 1), :] for p in range(4)]
        lo = jnp.where(subs8 < 4, rows[0], rows[1])
        hi = jnp.where(subs8 < 4, rows[2], rows[3])
        return jnp.concatenate([lo, hi], axis=0)

    def correct(layers, i_lo, i_hi, edge_rows, pick, dst):
        def row(i, y, fix, w):
            dst[w, rows_of(y), :] = pick(w, y) * fine_valid(y) + fix

        def body(i, carry):
            for w in layers:
                fix = correction(i, w)
                for q in range(4):
                    row(i, HY + (i - H1) * 4 + q, fix, w)
            return carry

        lax.fori_loop(i_lo, i_hi, body, 0)
        for y in edge_rows:
            i = (y - HY) // 4 + H1
            for w in layers:
                row(i, y, correction(i, w), w)

    arrived(near)
    start_from_zero(v0, own_layers, HY - 2, HY + ROWS + 2)
    start_from_zero(v0, [3, 8], HY - 1, HY + ROWS + 1)
    sweep(v0, v1, own_layers, HY - 1, HY + ROWS + 1)
    restricted_residual(v1, 0)

    def background_one():
        return [
            push(f.at[4, own], f.at[0, own], 1, 0),
            push(f.at[7, own], f.at[11, own], -1, 0),
            push(v1.at[4, own], v1.at[0, own], 1, 0),
            push(v1.at[7, own], v1.at[11, own], -1, 0),
            push(v1.at[4, rows_of(last)], v1.at[0, rows_of(HY - 1)], 1, 1),
            push(v1.at[4, rows_of(HY)], v1.at[0, rows_of(last + 1)], 1, -1),
            push(v1.at[7, rows_of(last)], v1.at[11, rows_of(HY - 1)], -1, 1),
            push(v1.at[7, rows_of(HY)], v1.at[11, rows_of(last + 1)], -1, -1),
        ]

    def forward_rows(extra):
        arrived(bulk)
        arrived(extra[0:2])
        hi, lo = last + 1 - HY, HY
        out = []
        for g in (0, 9):
            out.append(push(f.at[pl.ds(g, 3), rows_of(hi, HY)], f.at[pl.ds(g, 3), rows_of(0, HY)], 0, 1))
            out.append(push(f.at[pl.ds(g, 3), rows_of(lo, HY)], f.at[pl.ds(g, 3), rows_of(HY + ROWS, HY)], 0, -1))
        for w in (3, 8):
            out.append(push(f.at[w, rows_of(hi, HY - 1)], f.at[w, rows_of(0, HY - 1)], 0, 1))
            out.append(push(f.at[w, rows_of(lo + 1, HY - 1)], f.at[w, rows_of(HY + ROWS + 1, HY - 1)], 0, -1))
        return out

    extra = coarse_cycle(0, background_one, forward_rows)
    sent(extra[2:8])
    arrived(extra[2:])
    all_layers = list(range(NW))
    inner = list(range(1, NW - 1))
    start_from_zero(v0, all_layers, 0, NYW)
    sweep(v0, v1, inner, 1, NYW - 1)
    correct(all_layers, H1 - 1, H1 + 5, (1, NYW - 2), lambda w, y: v1[w, rows_of(y), :], v1)
    bufs = (v1, v0)
    for s in range(4):
        sweep(bufs[s % 2], bufs[(s + 1) % 2], list(range(s + 1, NW - 1 - s)), s + 2, NYW - 2 - s)
    restricted_residual(v1, 1)

    def background_two():
        return [
            push(v1.at[pl.ds(5, 3), own], v2.at[pl.ds(1, 3), own], 1, 0),
            push(v1.at[pl.ds(4, 3), own], v2.at[pl.ds(8, 3), own], -1, 0),
            push(v1.at[pl.ds(4, 4), rows_of(last - 2, 3)], v2.at[pl.ds(4, 4), rows_of(HY - 3, 3)], 0, 1),
            push(v1.at[pl.ds(4, 4), rows_of(HY, 3)], v2.at[pl.ds(4, 4), rows_of(last + 1, 3)], 0, -1),
            push(v1.at[pl.ds(6, 2), rows_of(last - 1, 2)], v2.at[pl.ds(2, 2), rows_of(HY - 2, 2)], 1, 1),
            push(v1.at[pl.ds(6, 2), rows_of(HY, 2)], v2.at[pl.ds(2, 2), rows_of(last + 1, 2)], 1, -1),
            push(v1.at[pl.ds(4, 2), rows_of(last - 1, 2)], v2.at[pl.ds(8, 2), rows_of(HY - 2, 2)], -1, 1),
            push(v1.at[pl.ds(4, 2), rows_of(HY, 2)], v2.at[pl.ds(8, 2), rows_of(last + 1, 2)], -1, -1),
        ]

    tail = coarse_cycle(1, background_two, lambda extra: [])
    arrived(tail)

    def keep_own(y, carry):
        for w in own_layers:
            v2[w, rows_of(y), :] = v1[w, rows_of(y), :]
        return carry

    lax.fori_loop(HY, HY + ROWS, keep_own, 0)
    deep = list(range(1, NW - 1))
    correct(deep, H1 - 1, H1 + 5, (), lambda w, y: v2[w, rows_of(y), :], v0)
    sent(tail)
    sweep(v0, v1, deep[1:-1], HY - 2, HY + ROWS + 2)
    sweep(v1, v0, deep[2:-2], HY - 1, HY + ROWS + 1)

    consts, _ = layer_consts(own_layers)

    def defect(y, carry):
        for w in own_layers:
            x, total = flows(v0, w, y, consts[w])
            v2[w, rows_of(y), :] = total - diagonal(w, y, consts[w]) * x
        return carry

    lax.fori_loop(HY, HY + ROWS, defect, 0)

    for src, out in ((v0, v_out), (v2, b_out)):
        for k in range(K):
            block = jnp.concatenate([src[w, pl.ds(HY * K + k, ROWS, stride=K), :] for w in own_layers], axis=0)
            turn[pl.ds(k, LANES, stride=K), 0:LZ * ROWS] = block.T
        for m in range(K):
            block = turn[m * LANES:(m + 1) * LANES, 0:LZ * ROWS].T
            out[:, :, m * LANES:(m + 1) * LANES] = block.reshape(LZ, ROWS, LANES)
    sent(par + near + bulk + extra[0:2] + extra[8:])


N_COPIES = 3 + 8 + 2 + 8 + 8 + 8 + 2 * (3 + 4 + 2 * H2)


def local(n_tile, source_heating, material_thermal_values, layer_material, via_conductance, via_blocks):
    onehot = (layer_material[:, None]
              == jnp.arange(material_thermal_values.shape[0], dtype=jnp.int32)[None, :]).astype(F32)
    layer_cond = jnp.sum(onehot * material_thermal_values[None, :], axis=1)
    blocks = via_blocks[0].astype(F32)
    pk = jnp.concatenate([
        jnp.pad(blocks, ((0, 0), (0, LANES - 4))),
        jnp.broadcast_to(layer_cond[:, None], (LZ, LANES)),
        jnp.broadcast_to(via_conductance[:, None], (1, LANES)),
        jnp.pad(blocks.T[0:3:2], ((0, 0), (0, LANES - blocks.shape[0]))),
        jnp.zeros((1, LANES), F32),
    ], axis=0)

    def tiles(*lead):
        return pltpu.VMEM(lead + (NZ, LANES), F32)

    def window(n):
        return pltpu.VMEM((n, NYW * K, LANES), F32)

    vmem = pl.BlockSpec(memory_space=pltpu.VMEM)
    shape = jax.ShapeDtypeStruct(source_heating.shape, F32)
    return pl.pallas_call(
        functools.partial(kernel, n_tile),
        out_shape=(shape, shape),
        in_specs=[vmem, vmem],
        out_specs=(vmem, vmem),
        scratch_shapes=[
            window(NW), window(NW), window(NW), window(NW), window(4),
            pltpu.VMEM((NYW * K, LANES), F32), window(3), window(3),
            pltpu.VMEM((4, 32, LANES), F32), tiles(2),
            pltpu.VMEM((K * LANES, LANES), F32), pltpu.VMEM((4 * 8 * K, LANES), F32),
            pltpu.VMEM((2, 4, 16, 8, LANES), F32), tiles(2, N1 * 4),
            tiles(N1 * 4), tiles(N1 * 4), tiles(N1 * 4), tiles(N1 * 4), tiles(N1 * 4),
            tiles(2, N2), tiles(N2), tiles(N2), tiles(N2), tiles(N2), tiles(N2),
            pltpu.VMEM((4, 80, LANES), F32),
            pltpu.SemaphoreType.DMA((N_COPIES,)),
            pltpu.SemaphoreType.DMA((N_COPIES,)),
        ],
        compiler_params=pltpu.CompilerParams(collective_id=0, has_side_effects=True),
    )(source_heating, pk)


def solution(mesh):
    in_specs = (P("die", "tile", None), P(), P("die"), P("die"), P("die", None, None))
    out_specs = (P("die", "tile", None), P("die", "tile", None))
    body = functools.partial(local, mesh.shape["tile"])
    return jax.shard_map(body, mesh=mesh, in_specs=in_specs, out_specs=out_specs, check_vma=False)
```

time: 566 us -> 93 us (0.16)
  the two profiles are of different devices: /device:TPU:26 before, /device:TPU:1 now
where the time goes in v1:
time: 93 us; the launch traced here: 92.8 us
  Pallas kernels  86.1 us (93%)
  local copies, waits for them, and re-layouts  5.21 us (6%)
  between operations  1.32 us (1%)
    pallas_call x1, Pallas kernels, local(): pl.pallas_call(functools.partial(kernel, n_tile), out_shape=(shape, shape...  86.1 us
    unnamed x10, local copies, waits for them, and re-layouts  3.8 us

profile of v1, /device:TPU:1, one launch (start us, length us, event | category | flops | bytes accessed | tf_op | source)
XLA Modules:
  0.0 92.8 jit_solution(13106102450784867853)
XLA Ops:
  1.3 0.0 copy-start.2
  1.3 0.0 copy-start.3
  1.3 0.6 copy-done.2
  1.9 0.0 copy-done.3
  1.9 0.0 copy-start.1
  2.0 0.2 select_reduce_fusion
  2.1 0.1 broadcast_in_dim.8
  2.2 0.4 copy-done.1
  2.7 0.1 copy.8
  2.8 1.2 %concatenate.3.pk = f32[32,128]{1,0:T(8,128)} concatenate(f32[24,128]{1,0:T(8,128)S(1)} %pad.8, f32[4,128]{1,0:T(4,128)S(1)} %broadcast_in_dim.8, f32[1,128]{1,0:T(1,128)S(1)} %broadcast_in_dim.10, f32[2,128]{1,0:T(2,128)S(1)} %pad.9, f32[1,128]{1,0:T(1,128)S(1)} %broadcast_in_dim.11), dimensions={0} | concatenate | bytes 32768 | tf_op jit(solution)/shard_map/concatenate | solution.py:534
  4.0 86.1 %shard_map.68 = (f32[4,16,2048]{2,1,0:T(8,128)}, f32[4,16,2048]{2,1,0:T(8,128)}) custom-call(f32[4,16,2048]{2,1,0:T(8,128)} %f_in.1, f32[32,128]{1,0:T(8,128)} %concatenate.3.pk), custom_call_target="tpu_custom_call" | custom-call | tf_op jit(solution)/shard_map/pallas_call | solution.py:550
  90.1 0.0 copy-start
  90.1 1.9 %copy.12 = f32[4,16,2048]{2,1,0:T(8,128)} copy(f32[4,16,2048]{2,1,0:T(8,128)} %get-tuple-element.6) | data formatting | bytes 1048576
  92.0 0.0 copy-done
  92.0 0.8 copy.13
  (6 shorter events, 0.1 us)
Async XLA Ops:
  1.3 0.7 copy-start.2
  1.3 0.7 copy-start.3
  1.9 0.7 copy-start.1
  90.1 1.9 %copy-start = (f32[4,16,2048]{2,1,0:T(8,128)S(1)}, f32[4,16,2048]{2,1,0:T(8,128)}, u32[]{:S(2)}) copy-start(f32[4,16,2048]{2,1,0:T(8,128)} %get-tuple-element.7) | copy-start | bytes 1572868

commit v2 on v1

v2 whole, which is shorter than its diff:
```python
import functools

import jax
import jax.numpy as jnp
from jax import lax
from jax.experimental import pallas as pl
from jax.experimental.pallas import tpu as pltpu
from jax.sharding import PartitionSpec as P

F32 = jnp.float32
OMEGA = 0.8
KEEP = 1.0 - OMEGA
LZ = 4
ROWS = 16
HY = 6
NYW = ROWS + 2 * HY
NW = 3 * LZ
K = 16
LANES = 128
H1 = 5
N1 = 4 + 2 * H1
H2 = 6
N2 = 1 + 2 * H2
NZ = 16


def rows_of(y, count=1):
    start = y * K
    if not isinstance(start, int):
        start = pl.multiple_of(start, K)
    return pl.ds(start, count * K)


def row_loop(lo, hi, unroll, fn):
    whole = (hi - lo) // unroll

    def body(i, carry):
        for j in range(unroll):
            fn(lo + i * unroll + j)
        return carry

    if whole:
        lax.fori_loop(0, whole, body, 0)
    for y in range(lo + whole * unroll, hi):
        fn(y)


def kernel(n_tile, f_in, mats, material, via_cond, blocks, v_out, b_out, f, v0, v1, v2, vn, vd_top, wlo, whi, pall, cz,
           turn, restr, r1g, r1, w1, u1, l1, a1, b1, r2, w2, u2, l2, a2, b2, via1, pk, send_sem, recv_sem):
    d = lax.axis_index("die")
    t = lax.axis_index("tile")

    def at(dd, dt):
        return {"die": lax.rem(d + dd + 4, 4), "tile": lax.rem(t + dt + n_tile, n_tile)}

    counter = [0]

    def push(src, dst, dd, dt):
        i = counter[0]
        counter[0] += 1
        copy = pltpu.make_async_remote_copy(
            src_ref=src, dst_ref=dst, send_sem=send_sem.at[i], recv_sem=recv_sem.at[i],
            device_id=at(dd, dt), device_id_type=pl.DeviceIdType.MESH)
        copy.start()
        return copy

    def arrived(copies):
        for copy in copies:
            copy.wait_recv()

    def sent(copies):
        for copy in copies:
            copy.wait_send()

    partners = [(1, 0), (2, 0), (3, 0), (1, 1), (1, -1), (-1, 1), (-1, -1)]
    partners += [(0, s * j) for j in range(1, H2 + 1) for s in (1, -1)]
    barrier = pltpu.get_barrier_semaphore()
    for dd, dt in partners:
        pl.semaphore_signal(barrier, inc=1, device_id=at(dd, dt), device_id_type=pl.DeviceIdType.MESH)

    for m in range(K):
        block = f_in[:, :, m * LANES:(m + 1) * LANES].reshape(LZ * ROWS, LANES)
        turn[m * LANES:(m + 1) * LANES, 0:LZ * ROWS] = block.T
    for k in range(K):
        block = turn[pl.ds(k, LANES, stride=K), 0:LZ * ROWS].T
        for z in range(LZ):
            f[LZ + z, pl.ds(HY * K + k, ROWS, stride=K), :] = block[z * ROWS:(z + 1) * ROWS]
    zero_row = jnp.zeros((K, LANES), F32)

    def clear(y):
        v1[0, rows_of(y), :] = zero_row
        v1[NW - 1, rows_of(y), :] = zero_row

    row_loop(0, NYW, 4, clear)

    pk[0:24, :] = jnp.zeros((24, LANES), F32)
    pk[0:24, 0:4] = blocks[0].astype(F32)
    along = pk[0:24, :].T
    for z in range(LZ):
        pk[24 + z:25 + z, :] = jnp.full((1, LANES), mats[material[z]], F32)
    pk[28:29, :] = jnp.full((1, LANES), via_cond[0], F32)
    pk[29:32, :] = jnp.zeros((3, LANES), F32)
    pk[29:30, 0:24] = along[0:1, :]
    pk[30:31, 0:24] = along[2:3, :]
    pall[d] = pk[...]

    def coverage(e, rows, row0, cell, lanes_cols):
        n_lanes = lanes_cols * LANES
        prm = pall[e]
        lane = lax.broadcasted_iota(jnp.int32, (24, n_lanes), 1)
        col = (((lane & (LANES - 1)) * lanes_cols + (lane >> 7)) * cell).astype(F32)
        c_lo, c_hi = prm[0:24, 1:2], prm[0:24, 1:2] + prm[0:24, 3:4]
        cols = jnp.maximum(jnp.minimum(c_hi, col + cell) - jnp.maximum(c_lo, col), 0.0)
        row = ((row0 + lax.broadcasted_iota(jnp.int32, (rows, LANES), 0)) * cell).astype(F32)
        r_lo, r_hi = prm[29:30, :], prm[29:30, :] + prm[30:31, :]
        cover = jnp.maximum(jnp.minimum(r_hi, row + cell) - jnp.maximum(r_lo, row), 0.0)
        return jnp.dot(cover[:, 0:24], cols, precision=lax.Precision.HIGHEST,
                       preferred_element_type=F32) * prm[28:29, 0:1]

    zs = lax.broadcasted_iota(jnp.int32, (NZ, LANES), 0)
    is_top = (zs & 3) == 3
    is_end = zs == NZ - 1
    lanes8 = lax.broadcasted_iota(jnp.int32, (8, LANES), 1)
    subs8 = lax.broadcasted_iota(jnp.int32, (8, LANES), 0)
    lanes16 = lax.broadcasted_iota(jnp.int32, (NZ, LANES), 1)

    def valid(row, count):
        return jnp.where((row >= 0) & (row < count), 1.0, 0.0).astype(F32)

    def fine_valid(y):
        return valid(t * ROWS - HY + y, n_tile * ROWS)

    def via_plane(j):
        plane = coverage(lax.rem(d + 2 + j, 4), 32, t * ROWS - HY, 1, K)
        for k in range(K):
            vn[j, pl.ds(k, NYW, stride=K), :] = plane[0:NYW, k * LANES:(k + 1) * LANES]

    via_plane(2)
    pl.semaphore_wait(barrier, len(partners))

    own = rows_of(HY, ROWS)
    last = HY + ROWS - 1
    par = [push(pk, pall.at[d], dd, 0) for dd in (1, 2, 3)]
    near = [
        push(f.at[7, own], f.at[3, own], 1, 0),
        push(f.at[4, own], f.at[8, own], -1, 0),
        push(f.at[pl.ds(4, 4), rows_of(last + 1 - HY, HY)], f.at[pl.ds(4, 4), rows_of(0, HY)], 0, 1),
        push(f.at[pl.ds(4, 4), rows_of(HY, HY)], f.at[pl.ds(4, 4), rows_of(HY + ROWS, HY)], 0, -1),
        push(f.at[7, rows_of(last)], f.at[3, rows_of(HY - 1)], 1, 1),
        push(f.at[7, rows_of(HY)], f.at[3, rows_of(last + 1)], 1, -1),
        push(f.at[4, rows_of(last)], f.at[8, rows_of(HY - 1)], -1, 1),
        push(f.at[4, rows_of(HY)], f.at[8, rows_of(last + 1)], -1, -1),
    ]
    bulk = [
        push(f.at[pl.ds(5, 2), own], f.at[pl.ds(1, 2), own], 1, 0),
        push(f.at[pl.ds(5, 2), own], f.at[pl.ds(9, 2), own], -1, 0),
    ]

    def clear_v2(y):
        for w in range(NW):
            v2[w, rows_of(y), :] = zero_row

    row_loop(0, NYW, 2, clear_v2)
    arrived(par)
    via_plane(1)

    cond = jnp.concatenate([pall[e, 24:28, :] for e in range(4)], axis=0)
    follow = jnp.concatenate([cond[1:], cond[NZ - 1:]], axis=0)
    vert = 2.0 * cond * follow / (cond + follow)
    cz[0] = cond
    cz[1] = vert

    def zrow(which, w):
        z = lax.rem(LZ * (d + 3) + w, NZ)
        return cz[which, pl.ds(z, 1), :]

    def splat(w):
        ty = w % LZ
        c = zrow(0, w)
        u = zrow(1, w) if ty < 3 else None
        lo = zrow(1, w - 1) if ty > 0 else None
        return c, u, lo

    edge = [jnp.where(lax.rem(d + 2 + j, 4) == 3, 0.0, 1.0).astype(F32) for j in range(4)]
    ends = [(splat(LZ * m), splat(LZ * m + 3)) for m in range(3)]

    def weight_below(m, y, ok, coupled):
        c, u, _ = ends[m][0]
        wlo[m, rows_of(y), :] = ok / (4.0 * c + u + coupled)

    def weight_above(m, y, ok, plane):
        c, _, lo = ends[m][1]
        whi[m, rows_of(y), :] = ok / (4.0 * c + lo + plane)

    def near_weights(y):
        ok = fine_valid(y) * OMEGA
        planes = {j: vn[j, rows_of(y), :] for j in (1, 2)}
        vd_top[rows_of(y), :] = planes[2]
        for j in (1, 2):
            coupled = planes[j] * edge[j]
            vn[j, rows_of(y), :] = coupled
            weight_below(j, y, ok, coupled)
            weight_above(j - 1, y, ok, planes[j])

    row_loop(0, NYW, 4, near_weights)

    def far_weights(y):
        ok = fine_valid(y) * OMEGA
        planes = {j: vn[j, rows_of(y), :] for j in (0, 3)}
        for j in (0, 3):
            vn[j, rows_of(y), :] = planes[j] * edge[j]
        weight_below(0, y, ok, planes[0] * edge[0])
        weight_above(2, y, ok, planes[3])

    def coarse_coeffs(via_rows, scale, couple, row_ok):
        via = jnp.zeros((NZ, LANES), F32)
        for e in range(4):
            via = jnp.where(zs == LZ * e + 3, via_rows[e], via)
        upper = jnp.where(is_top, via, vert * couple)
        nb = jnp.where(is_end, 0.0, upper)
        lower = pltpu.roll(nb, 1, 0)
        return (row_ok * OMEGA) / (4.0 * scale * cond + upper + lower), nb, lower

    def mid_coeffs(i):
        ok = valid(t * 4 - H1 + i, n_tile * 4)
        for p in range(4):
            got = coarse_coeffs([via1[e, pl.ds(p * 16 + i, 1), :] for e in range(4)], 4.0, 16.0, ok)
            w1[i * 4 + p], u1[i * 4 + p], l1[i * 4 + p] = got

    def low_coeffs(i):
        ok = valid(t - H2 + i, n_tile)
        got = coarse_coeffs([via1[e, pl.ds(64 + i, 1), :] for e in range(4)], 16.0, 256.0, ok)
        w2[i], u2[i], l2[i] = got

    def remaining_coefficients():
        for e in range(4):
            plane = coverage(e, 16, t * 4 - H1, 4, 4)
            for p in range(4):
                via1[e, p * 16:(p + 1) * 16, :] = plane[:, p * LANES:(p + 1) * LANES]
            via1[e, 64:80, :] = coverage(e, 16, t - H2, 16, 1)
        row_loop(0, N1, 2, mid_coeffs)
        row_loop(0, N2, 4, low_coeffs)
        via_plane(0)
        via_plane(3)
        row_loop(0, NYW, 4, far_weights)

    def beside(x):
        nxt = pltpu.roll(x, K - 1, 0)
        prv = pltpu.roll(x, 1, 0)
        n_lo, n_hi = nxt[0:8], nxt[8:16]
        p_lo, p_hi = prv[0:8], prv[8:16]
        n_in = jnp.where(lanes8 == LANES - 1, 0.0, pltpu.roll(n_hi, LANES - 1, 1))
        p_in = jnp.where(lanes8 == 0, 0.0, pltpu.roll(p_lo, 1, 1))
        n_hi = jnp.where(subs8 == 7, n_in, n_hi)
        p_lo = jnp.where(subs8 == 0, p_in, p_lo)
        return jnp.concatenate([n_lo + p_lo, n_hi + p_hi], axis=0)

    def flows(src, w, y, consts, above=True, below=True):
        c, u, lo = consts
        ty, m = w % LZ, w // LZ
        x = src[w, rows_of(y), :]
        side = (src[w, rows_of(y - 1), :] + src[w, rows_of(y + 1), :]) + beside(x)
        total = f[w, rows_of(y), :] + c * side
        if above:
            total += (vn[m + 1, rows_of(y), :] if ty == 3 else u) * src[w + 1, rows_of(y), :]
        if below:
            total += (vn[m, rows_of(y), :] if ty == 0 else lo) * src[w - 1, rows_of(y), :]
        return x, total

    def plain_weight(consts):
        c, u, lo = consts
        return OMEGA / (4.0 * c + u + lo)

    def weight(w, y, plain):
        ty, m = w % LZ, w // LZ
        if ty == 0:
            return wlo[m, rows_of(y), :]
        if ty == 3:
            return whi[m, rows_of(y), :]
        return plain * fine_valid(y)

    def layer_consts(layers):
        consts = {w: splat(w) for w in layers}
        plain = {w: plain_weight(consts[w]) for w in layers if w % LZ in (1, 2)}
        return consts, plain

    def start_from_zero(dst, layers, y_lo, y_hi):
        _, plain = layer_consts(layers)

        def body(y):
            for w in layers:
                dst[w, rows_of(y), :] = weight(w, y, plain.get(w)) * f[w, rows_of(y), :]

        row_loop(y_lo, y_hi, max(1, 16 // len(layers)), body)

    def unroll_of(layers, rows):
        return max(u for u in (1, 2, 3, 4) if rows % u == 0 and u * len(layers) <= 24)

    def sweep(src, dst, layers, y_lo, y_hi):
        consts, plain = layer_consts(layers)

        def body(y):
            for w in layers:
                x, total = flows(src, w, y, consts[w])
                dst[w, rows_of(y), :] = KEEP * x + weight(w, y, plain.get(w)) * total

        row_loop(y_lo, y_hi, unroll_of(layers, y_hi - y_lo), body)

    def diagonal(w, y, consts):
        c, u, lo = consts
        if w == LZ:
            return 4.0 * c + u + vn[1, rows_of(y), :]
        if w == LZ + 3:
            return 4.0 * c + lo + vd_top[rows_of(y), :]
        return 4.0 * c + u + lo

    own_layers = list(range(LZ, 2 * LZ))

    def restricted_residual(src, slot):
        consts, _ = layer_consts(own_layers)

        def body(i, carry):
            sums = [None] * 6
            for q in range(4):
                y = HY + i * 4 + q
                parts = []
                for w in own_layers:
                    x, total = flows(src, w, y, consts[w], above=w < LZ + 3, below=w > LZ)
                    parts.append(total - diagonal(w, y, consts[w]) * x)
                parts.append(vn[1, rows_of(y), :] * src[LZ, rows_of(y), :])
                parts.append(vn[2, rows_of(y), :] * src[LZ + 3, rows_of(y), :])
                sums = [p if s is None else s + p for s, p in zip(sums, parts)]
            for s in range(4):
                restr[pl.ds(pl.multiple_of((i * 4 + s) * K, K), K), :] = sums[s]
            for s in range(2):
                restr[pl.ds(pl.multiple_of(16 * K + (i * 2 + s) * K, K), K), :] = sums[4 + s]
            return carry

        lax.fori_loop(0, 4, body, 0)
        for g, start in enumerate((0, 16 * K, 8 * K)):
            for p in range(4):
                tile = restr[pl.ds(start + 4 * p, 8, stride=K), :]
                for q in range(1, 4):
                    tile += restr[pl.ds(start + 4 * p + q, 8, stride=K), :]
                r1g[slot, d, g * 4 + p] = tile

    mid_c = 4.0 * cond
    low_c = 16.0 * cond

    def lane_next(x):
        return jnp.where(lanes16 == LANES - 1, 0.0, pltpu.roll(x, LANES - 1, 1))

    def lane_prev(x):
        return jnp.where(lanes16 == 0, 0.0, pltpu.roll(x, 1, 1))

    def mid_flows(src, rhs, i):
        xs = [src[i * 4 + p] for p in range(4)]
        out = []
        for p in range(4):
            nxt = xs[p + 1] if p < 3 else lane_next(xs[0])
            prv = xs[p - 1] if p > 0 else lane_prev(xs[3])
            side = (src[i * 4 - 4 + p] + src[i * 4 + 4 + p]) + (nxt + prv)
            total = rhs[i * 4 + p] + mid_c * side
            total += u1[i * 4 + p] * pltpu.roll(xs[p], NZ - 1, 0)
            total += l1[i * 4 + p] * pltpu.roll(xs[p], 1, 0)
            out.append((xs[p], total))
        return out

    def mid_sweep(src, dst, rhs, lo, hi):
        def body(i):
            for p, (x, total) in enumerate(mid_flows(src, rhs, i)):
                dst[i * 4 + p] = KEEP * x + w1[i * 4 + p] * total

        row_loop(lo, hi, 2, body)

    def mid_start(rhs, lo, hi):
        def body(i):
            for p in range(4):
                a1[i * 4 + p] = w1[i * 4 + p] * rhs[i * 4 + p]

        row_loop(lo, hi, 2, body)

    def assemble(slot):
        def turned(x, shift):
            return x if shift % 8 == 0 else pltpu.roll(x, shift % 8, 0)

        for i in range(4):
            half = 4 * (i % 2)
            for p in range(4):
                ts = [r1g[slot, e, (0 if i < 2 else 8) + p] for e in range(4)]
                cs = [r1g[slot, e, 4 + p] for e in range(4)]

                def put(e, down, dst_row):
                    return jnp.where(subs8 == dst_row, turned(cs[e], dst_row - (2 * i + down)), 0.0)

                lo = jnp.where(subs8 < 4, turned(ts[0], -half), turned(ts[1], 4 - half))
                lo += put(1, 0, 3) + put(0, 1, 4) + put(2, 0, 7)
                hi = jnp.where(subs8 < 4, turned(ts[2], -half), turned(ts[3], 4 - half))
                hi += put(1, 1, 0) + put(3, 0, 3) + put(2, 1, 4)
                r1[slot, (H1 + i) * 4 + p] = jnp.concatenate([lo, hi], axis=0)

    def coarse_cycle(slot, after_gather, after_spread, while_waiting):
        gather = [push(r1g.at[slot, d], r1g.at[slot, d], dd, 0) for dd in (2, 1, 3)]
        after_gather()
        arrived(gather)
        assemble(slot)
        rhs = r1.at[slot]

        def mid_rows(i, count):
            return rhs.at[pl.ds(i * 4, count * 4)]

        urgent = [
            push(mid_rows(H1 + 2, 2), mid_rows(H1 - 2, 2), 0, 1),
            push(mid_rows(H1, 2), mid_rows(H1 + 4, 2), 0, -1),
        ]
        rest = [
            push(mid_rows(H1, 2), mid_rows(H1 - 4, 2), 0, 1),
            push(mid_rows(H1 + 2, 2), mid_rows(H1 + 6, 2), 0, -1),
            push(mid_rows(H1 + 3, 1), mid_rows(0, 1), 0, 2),
            push(mid_rows(H1, 1), mid_rows(N1 - 1, 1), 0, -2),
        ]
        after_spread()
        arrived(urgent)
        mid_start(rhs, H1 - 2, H1 + 6)
        mid_sweep(a1, b1, rhs, H1 - 1, H1 + 5)

        def down(i, acc):
            for j in range(2):
                row = H1 + 2 * i + j
                for p, (x, total) in enumerate(mid_flows(b1, rhs, row)):
                    acc += total - (OMEGA / w1[row * 4 + p]) * x
            return acc

        r2[slot, H2] = lax.fori_loop(0, 2, down, jnp.zeros((NZ, LANES), F32))
        low = []
        for j in range(H2, 0, -1):
            low.append(push(r2.at[slot, H2], r2.at[slot, H2 - j], 0, j))
            low.append(push(r2.at[slot, H2], r2.at[slot, H2 + j], 0, -j))
        arrived(rest)
        mid_start(rhs, 0, H1 - 2)
        mid_start(rhs, H1 + 6, N1)
        mid_sweep(a1, b1, rhs, 1, H1 - 1)
        mid_sweep(a1, b1, rhs, H1 + 5, N1 - 1)
        while_waiting()
        arrived(low)

        bufs = (a2, b2)
        for i in range(N2):
            a2[i] = w2[i] * r2[slot, i]
        for s in range(5):
            src, dst = bufs[s % 2], bufs[(s + 1) % 2]
            for i in range(s + 1, N2 - 1 - s):
                x = src[i]
                side = (src[i - 1] + src[i + 1]) + (lane_next(x) + lane_prev(x))
                total = r2[slot, i] + low_c * side
                total += u2[i] * pltpu.roll(x, NZ - 1, 0) + l2[i] * pltpu.roll(x, 1, 0)
                dst[i] = KEEP * x + w2[i] * total
        fix = bufs[1]
        for g in range(3):
            e2 = fix[H2 - 1 + g]
            for i in range(4):
                for p in range(4):
                    at_cell = (H1 - 4 + g * 4 + i) * 4 + p
                    b1[at_cell] = b1[at_cell] + e2
        mid_sweep(b1, a1, rhs, 2, N1 - 2)
        mid_sweep(a1, b1, rhs, 3, N1 - 3)
        sent(gather + urgent + rest + low)

    def correction(i, w):
        z = lax.rem(LZ * (d + 3) + w, NZ)
        rows = [b1[i * 4 + p, pl.ds(z, 1), :] for p in range(4)]
        lo = jnp.where(subs8 < 4, rows[0], rows[1])
        hi = jnp.where(subs8 < 4, rows[2], rows[3])
        return jnp.concatenate([lo, hi], axis=0)

    def correct(layers, i_lo, i_hi, edge_rows, pick, dst):
        def row(i, y, fix, w):
            dst[w, rows_of(y), :] = pick(w, y) * fine_valid(y) + fix

        def body(i):
            for w in layers:
                fix = correction(i, w)
                for q in range(4):
                    row(i, HY + (i - H1) * 4 + q, fix, w)

        row_loop(i_lo, i_hi, 1, body)
        for y in edge_rows:
            i = (y - HY) // 4 + H1
            for w in layers:
                row(i, y, correction(i, w), w)

    arrived(near)
    start_from_zero(v0, own_layers, HY - 2, HY + ROWS + 2)
    start_from_zero(v0, [3, 8], HY - 1, HY + ROWS + 1)
    sweep(v0, v1, own_layers, HY - 1, HY + ROWS + 1)
    restricted_residual(v1, 0)

    later = []
    forwarded = []
    far_source = []
    all_layers = list(range(NW))
    inner = list(range(1, NW - 1))

    def background_one():
        far_source.extend([
            push(f.at[4, own], f.at[0, own], 1, 0),
            push(f.at[7, own], f.at[11, own], -1, 0),
        ])
        later.extend([
            push(v1.at[4, own], v1.at[0, own], 1, 0),
            push(v1.at[7, own], v1.at[11, own], -1, 0),
            push(v1.at[4, rows_of(last)], v1.at[0, rows_of(HY - 1)], 1, 1),
            push(v1.at[4, rows_of(HY)], v1.at[0, rows_of(last + 1)], 1, -1),
            push(v1.at[7, rows_of(last)], v1.at[11, rows_of(HY - 1)], -1, 1),
            push(v1.at[7, rows_of(HY)], v1.at[11, rows_of(last + 1)], -1, -1),
        ])
        remaining_coefficients()

    def forward_rows():
        arrived(bulk + far_source)
        for far in range(1, 5):
            count = HY - far if far > 1 else HY - 2
            low_row, high_row = far, last + 1 + (1 if far == 1 else 0)
            for w in (LZ - far, 2 * LZ - 1 + far):
                forwarded.append(push(f.at[w, rows_of(low_row + ROWS, count)], f.at[w, rows_of(low_row, count)], 0, 1))
                forwarded.append(push(f.at[w, rows_of(high_row - ROWS, count)], f.at[w, rows_of(high_row, count)], 0, -1))

    def presmooth_window():
        arrived(forwarded)
        sent(later)
        start_from_zero(v0, all_layers, 0, NYW)
        sweep(v0, v1, inner, 1, NYW - 1)

    coarse_cycle(0, background_one, forward_rows, presmooth_window)
    arrived(later)
    correct(all_layers, H1 - 1, H1 + 5, (1, NYW - 2), lambda w, y: v1[w, rows_of(y), :], v1)
    bufs = (v1, v0)
    for s in range(4):
        sweep(bufs[s % 2], bufs[(s + 1) % 2], list(range(s + 1, NW - 1 - s)), s + 2, NYW - 2 - s)
    restricted_residual(v1, 1)

    tail = []

    def background_two():
        tail.extend([
            push(v1.at[pl.ds(5, 3), own], v2.at[pl.ds(1, 3), own], 1, 0),
            push(v1.at[pl.ds(4, 3), own], v2.at[pl.ds(8, 3), own], -1, 0),
            push(v1.at[pl.ds(4, 4), rows_of(last - 2, 3)], v2.at[pl.ds(4, 4), rows_of(HY - 3, 3)], 0, 1),
            push(v1.at[pl.ds(4, 4), rows_of(HY, 3)], v2.at[pl.ds(4, 4), rows_of(last + 1, 3)], 0, -1),
            push(v1.at[pl.ds(6, 2), rows_of(last - 1, 2)], v2.at[pl.ds(2, 2), rows_of(HY - 2, 2)], 1, 1),
            push(v1.at[pl.ds(6, 2), rows_of(HY, 2)], v2.at[pl.ds(2, 2), rows_of(last + 1, 2)], 1, -1),
            push(v1.at[pl.ds(4, 2), rows_of(last - 1, 2)], v2.at[pl.ds(8, 2), rows_of(HY - 2, 2)], -1, 1),
            push(v1.at[pl.ds(4, 2), rows_of(HY, 2)], v2.at[pl.ds(8, 2), rows_of(last + 1, 2)], -1, -1),
        ])

    coarse_cycle(1, background_two, lambda: None, lambda: None)
    arrived(tail)

    def keep_own(y):
        for w in own_layers:
            v2[w, rows_of(y), :] = v1[w, rows_of(y), :]

    row_loop(HY, HY + ROWS, 4, keep_own)
    deep = list(range(1, NW - 1))
    correct(deep, H1 - 1, H1 + 5, (), lambda w, y: v2[w, rows_of(y), :], v0)
    sent(tail)
    sweep(v0, v1, deep[1:-1], HY - 2, HY + ROWS + 2)
    sweep(v1, v0, deep[2:-2], HY - 1, HY + ROWS + 1)

    consts, _ = layer_consts(own_layers)

    def defect(y):
        for w in own_layers:
            x, total = flows(v0, w, y, consts[w])
            v2[w, rows_of(y), :] = total - diagonal(w, y, consts[w]) * x

    row_loop(HY, HY + ROWS, 4, defect)

    for src, out in ((v0, v_out), (v2, b_out)):
        for k in range(K):
            block = jnp.concatenate([src[w, pl.ds(HY * K + k, ROWS, stride=K), :] for w in own_layers], axis=0)
            turn[pl.ds(k, LANES, stride=K), 0:LZ * ROWS] = block.T
        for m in range(K):
            block = turn[m * LANES:(m + 1) * LANES, 0:LZ * ROWS].T
            out[:, :, m * LANES:(m + 1) * LANES] = block.reshape(LZ, ROWS, LANES)
    sent(par + near + bulk + far_source + forwarded)


N_COPIES = 3 + 8 + 2 + 8 + 16 + 8 + 2 * (3 + 6 + 2 * H2)


def local(n_tile, source_heating, material_thermal_values, layer_material, via_conductance, via_blocks):
    def tiles(*lead):
        return pltpu.VMEM(lead + (NZ, LANES), F32)

    def window(n):
        return pltpu.VMEM((n, NYW * K, LANES), F32)

    vmem = pl.BlockSpec(memory_space=pltpu.VMEM)
    smem = pl.BlockSpec(memory_space=pltpu.SMEM)
    shape = jax.ShapeDtypeStruct(source_heating.shape, F32)
    return pl.pallas_call(
        functools.partial(kernel, n_tile),
        out_shape=(shape, shape),
        in_specs=[vmem, smem, smem, smem, vmem],
        out_specs=(vmem, vmem),
        scratch_shapes=[
            window(NW), window(NW), window(NW), window(NW), window(4),
            pltpu.VMEM((NYW * K, LANES), F32), window(3), window(3),
            pltpu.VMEM((4, 32, LANES), F32), tiles(2),
            pltpu.VMEM((K * LANES, LANES), F32), pltpu.VMEM((4 * 6 * K, LANES), F32),
            pltpu.VMEM((2, 4, 12, 8, LANES), F32), tiles(2, N1 * 4),
            tiles(N1 * 4), tiles(N1 * 4), tiles(N1 * 4), tiles(N1 * 4), tiles(N1 * 4),
            tiles(2, N2), tiles(N2), tiles(N2), tiles(N2), tiles(N2), tiles(N2),
            pltpu.VMEM((4, 80, LANES), F32), pltpu.VMEM((32, LANES), F32),
            pltpu.SemaphoreType.DMA((N_COPIES,)),
            pltpu.SemaphoreType.DMA((N_COPIES,)),
        ],
        compiler_params=pltpu.CompilerParams(collective_id=0, has_side_effects=True),
    )(source_heating, material_thermal_values, layer_material, via_conductance, via_blocks)


def solution(mesh):
    in_specs = (P("die", "tile", None), P(), P("die"), P("die"), P("die", None, None))
    out_specs = (P("die", "tile", None), P("die", "tile", None))
    body = functools.partial(local, mesh.shape["tile"])
    return jax.shard_map(body, mesh=mesh, in_specs=in_specs, out_specs=out_specs, check_vma=False)
```

time: 93 us -> 73.1 us (0.79)
  Pallas kernels: 86.1 us -> 67.5 us
  local copies, waits for them, and re-layouts: 5.21 us -> 4.09 us
    pallas_call x1, Pallas kernels: 86.1 us -> 67.5 us  [local(): pl.pallas_call(functools.partial(kernel, n_tile), out_shape=(shape, shape...]
    concatenate x1 -> x0, local copies, waits for them, and re-layouts: 1.21 us -> none  [local(): jnp.concatenate([jnp.pad(blocks, ((0, 0), (0, LANES - 4))), jnp.broadcast...]
    unnamed x10 -> x5, local copies, waits for them, and re-layouts: 3.8 us -> 4.09 us
where the time goes in v2:
time: 73.1 us; the launch traced here: 72.9 us
  Pallas kernels  67.5 us (92%)
  local copies, waits for them, and re-layouts  4.09 us (6%)
  between operations  1.29 us (2%)
    pallas_call x1, Pallas kernels, local(): pl.pallas_call(functools.partial(kernel, n_tile), out_shape=(shape, shape...  67.5 us
    unnamed x5, local copies, waits for them, and re-layouts  4.09 us

profile of v2, /device:TPU:1, one launch (start us, length us, event | category | flops | bytes accessed | tf_op | source)
XLA Modules:
  0.0 72.9 jit_solution(10194100903479030966)
XLA Ops:
  1.3 1.4 %copy.7.blocks = s32[1,24,4]{2,1,0:T(8,128)} copy(s32[1,24,4]{1,2,0:T(4,128)} %param.9) | data formatting | bytes 768 | tf_op args[4]
  2.6 67.5 %shard_map.68 = (f32[4,16,2048]{2,1,0:T(8,128)}, f32[4,16,2048]{2,1,0:T(8,128)}) custom-call(f32[4,16,2048]{2,1,0:T(8,128)} %f_in.1, f32[6]{0:T(128)} %mats.1, s32[4]{0:T(128)} %material.1, f32[1]{0:T(128)S(6)} %copy.10.via_cond, s32[1,24,4]{2,1,0:T(8,128)} %copy.7.blocks), custom_call_target="tpu_custom_call" | custom-call | tf_op jit(solution)/shard_map/pallas_call | solution.py:602
  70.2 0.0 copy-start
  70.2 1.9 %copy.11 = f32[4,16,2048]{2,1,0:T(8,128)} copy(f32[4,16,2048]{2,1,0:T(8,128)} %get-tuple-element.4) | data formatting | bytes 1048576
  72.1 0.0 copy-done
  72.1 0.8 %copy.12 = f32[4,16,2048]{2,1,0:T(8,128)} copy(f32[4,16,2048]{2,1,0:T(8,128)S(1)} %copy-done) | data formatting | bytes 1048576
Async XLA Ops:
  70.2 1.9 %copy-start = (f32[4,16,2048]{2,1,0:T(8,128)S(1)}, f32[4,16,2048]{2,1,0:T(8,128)}, u32[]{:S(2)}) copy-start(f32[4,16,2048]{2,1,0:T(8,128)} %get-tuple-element.5) | copy-start | bytes 1572868

commit v3 on v2

--- a/solution.py
+++ b/solution.py
@@ -45,8 +45,8 @@
         fn(y)
 
 
-def kernel(n_tile, f_in, mats, material, via_cond, blocks, v_out, b_out, f, v0, v1, v2, vn, vd_top, wlo, whi, pall, cz,
-           turn, restr, r1g, r1, w1, u1, l1, a1, b1, r2, w2, u2, l2, a2, b2, via1, pk, send_sem, recv_sem):
+def kernel(n_tile, f_in, mats, material, via_cond, blocks, out, f_vm, f, v0, v1, v2, vn, vd_top, wlo, whi, pall, cz,
+           turn, restr, r1g, r1, w1, u1, l1, a1, b1, r2, w2, u2, l2, a2, b2, via1, pk, send_sem, recv_sem, in_sem):
     d = lax.axis_index("die")
     t = lax.axis_index("tile")
 
@@ -72,15 +72,23 @@
         for copy in copies:
             copy.wait_send()
 
+    loads = []
+    for g in range(4):
+        part = (slice(None), slice(None), pl.ds(g * 4 * LANES, 4 * LANES))
+        loads.append(pltpu.make_async_copy(f_in.at[part], f_vm.at[part], in_sem.at[g]))
+        loads[g].start()
+
     partners = [(1, 0), (2, 0), (3, 0), (1, 1), (1, -1), (-1, 1), (-1, -1)]
     partners += [(0, s * j) for j in range(1, H2 + 1) for s in (1, -1)]
     barrier = pltpu.get_barrier_semaphore()
     for dd, dt in partners:
         pl.semaphore_signal(barrier, inc=1, device_id=at(dd, dt), device_id_type=pl.DeviceIdType.MESH)
 
-    for m in range(K):
-        block = f_in[:, :, m * LANES:(m + 1) * LANES].reshape(LZ * ROWS, LANES)
-        turn[m * LANES:(m + 1) * LANES, 0:LZ * ROWS] = block.T
+    for g in range(4):
+        loads[g].wait()
+        for m in range(4 * g, 4 * g + 4):
+            block = f_vm[:, :, m * LANES:(m + 1) * LANES].reshape(LZ * ROWS, LANES)
+            turn[m * LANES:(m + 1) * LANES, 0:LZ * ROWS] = block.T
     for k in range(K):
         block = turn[pl.ds(k, LANES, stride=K), 0:LZ * ROWS].T
         for z in range(LZ):
@@ -93,29 +101,25 @@
 
     row_loop(0, NYW, 4, clear)
 
-    pk[0:24, :] = jnp.zeros((24, LANES), F32)
-    pk[0:24, 0:4] = blocks[0].astype(F32)
-    along = pk[0:24, :].T
+    pk[0:4, :] = jnp.full((4, LANES), via_cond[0], F32)
+    pk[0:4, 0:24] = blocks[0].astype(F32)
     for z in range(LZ):
-        pk[24 + z:25 + z, :] = jnp.full((1, LANES), mats[material[z]], F32)
-    pk[28:29, :] = jnp.full((1, LANES), via_cond[0], F32)
-    pk[29:32, :] = jnp.zeros((3, LANES), F32)
-    pk[29:30, 0:24] = along[0:1, :]
-    pk[30:31, 0:24] = along[2:3, :]
+        pk[4 + z:5 + z, :] = jnp.full((1, LANES), mats[material[z]], F32)
     pall[d] = pk[...]
 
     def coverage(e, rows, row0, cell, lanes_cols):
         n_lanes = lanes_cols * LANES
         prm = pall[e]
+        down = prm.T
         lane = lax.broadcasted_iota(jnp.int32, (24, n_lanes), 1)
         col = (((lane & (LANES - 1)) * lanes_cols + (lane >> 7)) * cell).astype(F32)
-        c_lo, c_hi = prm[0:24, 1:2], prm[0:24, 1:2] + prm[0:24, 3:4]
+        c_lo, c_hi = down[0:24, 1:2], down[0:24, 1:2] + down[0:24, 3:4]
         cols = jnp.maximum(jnp.minimum(c_hi, col + cell) - jnp.maximum(c_lo, col), 0.0)
         row = ((row0 + lax.broadcasted_iota(jnp.int32, (rows, LANES), 0)) * cell).astype(F32)
-        r_lo, r_hi = prm[29:30, :], prm[29:30, :] + prm[30:31, :]
+        r_lo, r_hi = prm[0:1, :], prm[0:1, :] + prm[2:3, :]
         cover = jnp.maximum(jnp.minimum(r_hi, row + cell) - jnp.maximum(r_lo, row), 0.0)
         return jnp.dot(cover[:, 0:24], cols, precision=lax.Precision.HIGHEST,
-                       preferred_element_type=F32) * prm[28:29, 0:1]
+                       preferred_element_type=F32) * prm[0:1, LANES - 1:]
 
     zs = lax.broadcasted_iota(jnp.int32, (NZ, LANES), 0)
     is_top = (zs & 3) == 3
@@ -164,7 +168,7 @@
     arrived(par)
     via_plane(1)
 
-    cond = jnp.concatenate([pall[e, 24:28, :] for e in range(4)], axis=0)
+    cond = jnp.concatenate([pall[e, 4:8, :] for e in range(4)], axis=0)
     follow = jnp.concatenate([cond[1:], cond[NZ - 1:]], axis=0)
     vert = 2.0 * cond * follow / (cond + follow)
     cz[0] = cond
@@ -294,7 +298,7 @@
         row_loop(y_lo, y_hi, max(1, 16 // len(layers)), body)
 
     def unroll_of(layers, rows):
-        return max(u for u in (1, 2, 3, 4) if rows % u == 0 and u * len(layers) <= 24)
+        return max(u for u in (1, 2, 3, 4, 6) if rows % u == 0 and u * len(layers) <= 24)
 
     def sweep(src, dst, layers, y_lo, y_hi):
         consts, plain = layer_consts(layers)
@@ -371,7 +375,7 @@
             for p, (x, total) in enumerate(mid_flows(src, rhs, i)):
                 dst[i * 4 + p] = KEEP * x + w1[i * 4 + p] * total
 
-        row_loop(lo, hi, 2, body)
+        row_loop(lo, hi, max(u for u in (1, 2, 3, 4, 5) if (hi - lo) % u == 0), body)
 
     def mid_start(rhs, lo, hi):
         def body(i):
@@ -576,14 +580,18 @@
 
     row_loop(HY, HY + ROWS, 4, defect)
 
-    for src, out in ((v0, v_out), (v2, b_out)):
-        for k in range(K):
-            block = jnp.concatenate([src[w, pl.ds(HY * K + k, ROWS, stride=K), :] for w in own_layers], axis=0)
-            turn[pl.ds(k, LANES, stride=K), 0:LZ * ROWS] = block.T
-        for m in range(K):
-            block = turn[m * LANES:(m + 1) * LANES, 0:LZ * ROWS].T
-            out[:, :, m * LANES:(m + 1) * LANES] = block.reshape(LZ, ROWS, LANES)
+    for k in range(K):
+        block = jnp.concatenate([src[w, pl.ds(HY * K + k, ROWS, stride=K), :]
+                                 for src in (v0, v2) for w in own_layers], axis=0)
+        out[pl.ds(k, LANES, stride=K), :] = block.T
     sent(par + near + bulk + far_source + forwarded)
+
+
+def natural(turned, v_out, b_out):
+    for m in range(turned.shape[0] // LANES):
+        block = turned[m * LANES:(m + 1) * LANES, :].T
+        v_out[:, :, m * LANES:(m + 1) * LANES] = block[0:LZ * ROWS].reshape(LZ, ROWS, LANES)
+        b_out[:, :, m * LANES:(m + 1) * LANES] = block[LZ * ROWS:].reshape(LZ, ROWS, LANES)
 
 
 N_COPIES = 3 + 8 + 2 + 8 + 16 + 8 + 2 * (3 + 6 + 2 * H2)
@@ -599,25 +607,37 @@
     vmem = pl.BlockSpec(memory_space=pltpu.VMEM)
     smem = pl.BlockSpec(memory_space=pltpu.SMEM)
     shape = jax.ShapeDtypeStruct(source_heating.shape, F32)
-    return pl.pallas_call(
+    turned = pl.pallas_call(
         functools.partial(kernel, n_tile),
-        out_shape=(shape, shape),
-        in_specs=[vmem, smem, smem, smem, vmem],
-        out_specs=(vmem, vmem),
+        out_shape=jax.ShapeDtypeStruct((K * LANES, LANES), F32),
+        in_specs=[pl.BlockSpec(memory_space=pl.ANY), smem, smem, smem, vmem],
+        out_specs=vmem,
         scratch_shapes=[
+            pltpu.VMEM(source_heating.shape, F32),
             window(NW), window(NW), window(NW), window(NW), window(4),
             pltpu.VMEM((NYW * K, LANES), F32), window(3), window(3),
-            pltpu.VMEM((4, 32, LANES), F32), tiles(2),
+            pltpu.VMEM((4, 8, LANES), F32), tiles(2),
             pltpu.VMEM((K * LANES, LANES), F32), pltpu.VMEM((4 * 6 * K, LANES), F32),
             pltpu.VMEM((2, 4, 12, 8, LANES), F32), tiles(2, N1 * 4),
             tiles(N1 * 4), tiles(N1 * 4), tiles(N1 * 4), tiles(N1 * 4), tiles(N1 * 4),
             tiles(2, N2), tiles(N2), tiles(N2), tiles(N2), tiles(N2), tiles(N2),
-            pltpu.VMEM((4, 80, LANES), F32), pltpu.VMEM((32, LANES), F32),
+            pltpu.VMEM((4, 80, LANES), F32), pltpu.VMEM((8, LANES), F32),
             pltpu.SemaphoreType.DMA((N_COPIES,)),
             pltpu.SemaphoreType.DMA((N_COPIES,)),
+            pltpu.SemaphoreType.DMA((4,)),
         ],
         compiler_params=pltpu.CompilerParams(collective_id=0, has_side_effects=True),
-    )(source_heating, material_thermal_values, layer_material, via_conductance, via_blocks)
+    )(source_heating, material_thermal_values, layer_material, via_conductance, via_blocks.transpose(0, 2, 1))
+    steps = 4
+    chunk = K * LANES // steps
+    whole = pl.BlockSpec((LZ, ROWS, chunk), lambda i: (0, 0, i))
+    return pl.pallas_call(
+        natural,
+        grid=(steps,),
+        out_shape=(shape, shape),
+        in_specs=[pl.BlockSpec((chunk, LANES), lambda i: (i, 0))],
+        out_specs=(whole, whole),
+    )(turned)
 
 
 def solution(mesh):

time: 73.1 us -> 70.1 us (0.959)
  local copies, waits for them, and re-layouts: 4.09 us -> 0 us
  Pallas kernels: 67.5 us -> 68.6 us
    unnamed x5 -> x0, local copies, waits for them, and re-layouts: 4.09 us -> none
    pallas_call x1 -> x2, Pallas kernels: 67.5 us -> 68.6 us  [the longest x1 65 us: local(): pl.pallas_call(functools.partial(kernel, n_tile), out_shape=jax.ShapeDtyp...]
where the time goes in v3:
time: 70.1 us; the launch traced here: 69.9 us
  Pallas kernels  68.6 us (98%)
  between operations  1.28 us (2%)
    pallas_call x1, Pallas kernels, local(): pl.pallas_call(functools.partial(kernel, n_tile), out_shape=jax.ShapeDtyp...  65 us
    pallas_call x1, Pallas kernels, local(): pl.pallas_call(natural, grid=(steps,), out_shape=(shape, shape), in_specs...  3.56 us

profile of v3, /device:TPU:1, one launch (start us, length us, event | category | flops | bytes accessed | tf_op | source)
XLA Modules:
  0.0 69.9 jit_solution(14574452743111190931)
XLA Ops:
  1.3 65.0 %shard_map.68.turned = f32[2048,128]{1,0:T(8,128)} custom-call(f32[4,16,2048]{2,1,0:T(8,128)} %f_in.1, f32[6]{0:T(128)} %mats.1, s32[4]{0:T(128)} %material.1, f32[1]{0:T(128)S(6)} %copy.7.via_cond, s32[1,4,24]{2,1,0:T(4,128)} %bitcast.1), custom_call_target="tpu_custom_call" | custom-call | tf_op jit(solution)/shard_map/pallas_call | solution.py:610
  66.3 3.6 %shard_map.69 = (f32[4,16,2048]{2,1,0:T(8,128)}, f32[4,16,2048]{2,1,0:T(8,128)}) custom-call(f32[2048,128]{1,0:T(8,128)} %shard_map.68.turned), custom_call_target="tpu_custom_call" | custom-call | tf_op jit(solution)/shard_map/pallas_call | solution.py:634

commit v4 on v3

--- a/solution.py
+++ b/solution.py
@@ -45,7 +45,7 @@
         fn(y)
 
 
-def kernel(n_tile, f_in, mats, material, via_cond, blocks, out, f_vm, f, v0, v1, v2, vn, vd_top, wlo, whi, pall, cz,
+def kernel(n_tile, f_in, mats_in, material_in, via_cond_in, blocks_in, out, mats, material, via_cond, blocks, f_vm, f, v0, v1, v2, vn, vd_top, wlo, whi, pall, cz,
            turn, restr, r1g, r1, w1, u1, l1, a1, b1, r2, w2, u2, l2, a2, b2, via1, pk, send_sem, recv_sem, in_sem):
     d = lax.axis_index("die")
     t = lax.axis_index("tile")
@@ -77,6 +77,11 @@
         part = (slice(None), slice(None), pl.ds(g * 4 * LANES, 4 * LANES))
         loads.append(pltpu.make_async_copy(f_in.at[part], f_vm.at[part], in_sem.at[g]))
         loads[g].start()
+
+    small = []
+    for g, (src, dst) in enumerate(((mats_in, mats), (material_in, material), (via_cond_in, via_cond), (blocks_in, blocks))):
+        small.append(pltpu.make_async_copy(src, dst, in_sem.at[4 + g]))
+        small[g].start()
 
     partners = [(1, 0), (2, 0), (3, 0), (1, 1), (1, -1), (-1, 1), (-1, -1)]
     partners += [(0, s * j) for j in range(1, H2 + 1) for s in (1, -1)]
@@ -96,11 +101,13 @@
     zero_row = jnp.zeros((K, LANES), F32)
 
     def clear(y):
-        v1[0, rows_of(y), :] = zero_row
-        v1[NW - 1, rows_of(y), :] = zero_row
+        for w in (0, 1, NW - 2, NW - 1):
+            v1[w, rows_of(y), :] = zero_row
 
     row_loop(0, NYW, 4, clear)
 
+    for copy in small:
+        copy.wait()
     pk[0:4, :] = jnp.full((4, LANES), via_cond[0], F32)
     pk[0:4, 0:24] = blocks[0].astype(F32)
     for z in range(LZ):
@@ -156,8 +163,10 @@
         push(f.at[4, rows_of(HY)], f.at[8, rows_of(last + 1)], -1, -1),
     ]
     bulk = [
-        push(f.at[pl.ds(5, 2), own], f.at[pl.ds(1, 2), own], 1, 0),
-        push(f.at[pl.ds(5, 2), own], f.at[pl.ds(9, 2), own], -1, 0),
+        push(f.at[6, own], f.at[2, own], 1, 0),
+        push(f.at[5, own], f.at[9, own], -1, 0),
+        push(f.at[5, rows_of(HY, 8)], f.at[1, rows_of(HY, 8)], 1, 0),
+        push(f.at[6, rows_of(HY, 8)], f.at[10, rows_of(HY, 8)], -1, 0),
     ]
 
     def clear_v2(y):
@@ -493,10 +502,12 @@
             for w in layers:
                 row(i, y, correction(i, w), w)
 
-    arrived(near)
+    arrived(near[2:4])
     start_from_zero(v0, own_layers, HY - 2, HY + ROWS + 2)
+    sweep(v0, v1, [5, 6], HY - 1, HY + ROWS + 1)
+    arrived(near[0:2] + near[4:])
     start_from_zero(v0, [3, 8], HY - 1, HY + ROWS + 1)
-    sweep(v0, v1, own_layers, HY - 1, HY + ROWS + 1)
+    sweep(v0, v1, [4, 7], HY - 1, HY + ROWS + 1)
     restricted_residual(v1, 0)
 
     later = []
@@ -507,35 +518,51 @@
 
     def background_one():
         far_source.extend([
-            push(f.at[4, own], f.at[0, own], 1, 0),
-            push(f.at[7, own], f.at[11, own], -1, 0),
+            push(f.at[5, rows_of(HY + 8, 8)], f.at[1, rows_of(HY + 8, 8)], 1, 0),
+            push(f.at[6, rows_of(HY + 8, 8)], f.at[10, rows_of(HY + 8, 8)], -1, 0),
         ])
         later.extend([
-            push(v1.at[4, own], v1.at[0, own], 1, 0),
-            push(v1.at[7, own], v1.at[11, own], -1, 0),
-            push(v1.at[4, rows_of(last)], v1.at[0, rows_of(HY - 1)], 1, 1),
-            push(v1.at[4, rows_of(HY)], v1.at[0, rows_of(last + 1)], 1, -1),
-            push(v1.at[7, rows_of(last)], v1.at[11, rows_of(HY - 1)], -1, 1),
-            push(v1.at[7, rows_of(HY)], v1.at[11, rows_of(last + 1)], -1, -1),
+            push(v1.at[pl.ds(4, 2), own], v1.at[pl.ds(0, 2), own], 1, 0),
+            push(v1.at[pl.ds(6, 2), own], v1.at[pl.ds(10, 2), own], -1, 0),
+            push(v1.at[pl.ds(4, 2), rows_of(last - 1, 2)], v1.at[pl.ds(0, 2), rows_of(HY - 2, 2)], 1, 1),
+            push(v1.at[pl.ds(4, 2), rows_of(HY, 2)], v1.at[pl.ds(0, 2), rows_of(last + 1, 2)], 1, -1),
+            push(v1.at[pl.ds(6, 2), rows_of(last - 1, 2)], v1.at[pl.ds(10, 2), rows_of(HY - 2, 2)], -1, 1),
+            push(v1.at[pl.ds(6, 2), rows_of(HY, 2)], v1.at[pl.ds(10, 2), rows_of(last + 1, 2)], -1, -1),
         ])
         remaining_coefficients()
-
-    def forward_rows():
-        arrived(bulk + far_source)
-        for far in range(1, 5):
-            count = HY - far if far > 1 else HY - 2
-            low_row, high_row = far, last + 1 + (1 if far == 1 else 0)
-            for w in (LZ - far, 2 * LZ - 1 + far):
-                forwarded.append(push(f.at[w, rows_of(low_row + ROWS, count)], f.at[w, rows_of(low_row, count)], 0, 1))
-                forwarded.append(push(f.at[w, rows_of(high_row - ROWS, count)], f.at[w, rows_of(high_row, count)], 0, -1))
+        arrived(bulk)
+        forward(1)
+        forward(2)
+
+    def forward(far):
+        count = HY - far if far > 1 else HY - 2
+        low_row, high_row = far, last + 1 + (1 if far == 1 else 0)
+        for w in (LZ - far, 2 * LZ - 1 + far):
+            forwarded.append(push(f.at[w, rows_of(low_row + ROWS, count)], f.at[w, rows_of(low_row, count)], 0, 1))
+            forwarded.append(push(f.at[w, rows_of(high_row - ROWS, count)], f.at[w, rows_of(high_row, count)], 0, -1))
+
+    outer = [2, 3, 8, 9]
+
+    def forward_last():
+        arrived(far_source)
+        forward(3)
+
+    def window_inside():
+        start_from_zero(v0, [1, 2, 3, 8, 9, 10], HY, HY + ROWS)
+        sweep(v0, v1, outer, HY + 1, HY + ROWS - 1)
 
     def presmooth_window():
+        window_inside()
         arrived(forwarded)
         sent(later)
-        start_from_zero(v0, all_layers, 0, NYW)
-        sweep(v0, v1, inner, 1, NYW - 1)
-
-    coarse_cycle(0, background_one, forward_rows, presmooth_window)
+        for lo, hi in ((0, HY), (HY + ROWS, NYW)):
+            start_from_zero(v0, inner, lo, hi)
+        sweep(v0, v1, own_layers, 1, HY - 1)
+        sweep(v0, v1, own_layers, HY + ROWS + 1, NYW - 1)
+        sweep(v0, v1, outer, 1, HY + 1)
+        sweep(v0, v1, outer, HY + ROWS - 1, NYW - 1)
+
+    coarse_cycle(0, background_one, forward_last, presmooth_window)
     arrived(later)
     correct(all_layers, H1 - 1, H1 + 5, (1, NYW - 2), lambda w, y: v1[w, rows_of(y), :], v1)
     bufs = (v1, v0)
@@ -587,14 +614,32 @@
     sent(par + near + bulk + far_source + forwarded)
 
 
-def natural(turned, v_out, b_out):
-    for m in range(turned.shape[0] // LANES):
-        block = turned[m * LANES:(m + 1) * LANES, :].T
-        v_out[:, :, m * LANES:(m + 1) * LANES] = block[0:LZ * ROWS].reshape(LZ, ROWS, LANES)
-        b_out[:, :, m * LANES:(m + 1) * LANES] = block[LZ * ROWS:].reshape(LZ, ROWS, LANES)
-
-
-N_COPIES = 3 + 8 + 2 + 8 + 16 + 8 + 2 * (3 + 6 + 2 * H2)
+OUT_PARTS = 4
+
+
+def natural(turned_in, v_out, b_out, turned, v_vm, b_vm, sem):
+    copies = []
+    per = K // OUT_PARTS
+    loads = []
+    for g in range(OUT_PARTS):
+        part = pl.ds(g * per * LANES, per * LANES)
+        loads.append(pltpu.make_async_copy(turned_in.at[part], turned.at[part], sem.at[2, g]))
+        loads[g].start()
+    for g in range(OUT_PARTS):
+        loads[g].wait()
+        for m in range(g * per, (g + 1) * per):
+            block = turned[m * LANES:(m + 1) * LANES, :].T
+            v_vm[:, :, m * LANES:(m + 1) * LANES] = block[0:LZ * ROWS].reshape(LZ, ROWS, LANES)
+            b_vm[:, :, m * LANES:(m + 1) * LANES] = block[LZ * ROWS:].reshape(LZ, ROWS, LANES)
+        part = (slice(None), slice(None), pl.ds(g * per * LANES, per * LANES))
+        for i, (src, dst) in enumerate(((v_vm, v_out), (b_vm, b_out))):
+            copies.append(pltpu.make_async_copy(src.at[part], dst.at[part], sem.at[i, g]))
+            copies[-1].start()
+    for copy in copies:
+        copy.wait()
+
+
+N_COPIES = 3 + 8 + 4 + 8 + 12 + 8 + 2 * (3 + 6 + 2 * H2)
 
 
 def local(n_tile, source_heating, material_thermal_values, layer_material, via_conductance, via_blocks):
@@ -605,14 +650,15 @@
         return pltpu.VMEM((n, NYW * K, LANES), F32)
 
     vmem = pl.BlockSpec(memory_space=pltpu.VMEM)
-    smem = pl.BlockSpec(memory_space=pltpu.SMEM)
     shape = jax.ShapeDtypeStruct(source_heating.shape, F32)
     turned = pl.pallas_call(
         functools.partial(kernel, n_tile),
         out_shape=jax.ShapeDtypeStruct((K * LANES, LANES), F32),
-        in_specs=[pl.BlockSpec(memory_space=pl.ANY), smem, smem, smem, vmem],
+        in_specs=[pl.BlockSpec(memory_space=pltpu.HBM)] * 5,
         out_specs=vmem,
         scratch_shapes=[
+            pltpu.SMEM(material_thermal_values.shape, F32), pltpu.SMEM(layer_material.shape, jnp.int32),
+            pltpu.SMEM(via_conductance.shape, F32), pltpu.VMEM((1, 4, via_blocks.shape[1]), jnp.int32),
             pltpu.VMEM(source_heating.shape, F32),
             window(NW), window(NW), window(NW), window(NW), window(4),
             pltpu.VMEM((NYW * K, LANES), F32), window(3), window(3),
@@ -624,19 +670,18 @@
             pltpu.VMEM((4, 80, LANES), F32), pltpu.VMEM((8, LANES), F32),
             pltpu.SemaphoreType.DMA((N_COPIES,)),
             pltpu.SemaphoreType.DMA((N_COPIES,)),
-            pltpu.SemaphoreType.DMA((4,)),
+            pltpu.SemaphoreType.DMA((8,)),
         ],
         compiler_params=pltpu.CompilerParams(collective_id=0, has_side_effects=True),
     )(source_heating, material_thermal_values, layer_material, via_conductance, via_blocks.transpose(0, 2, 1))
-    steps = 4
-    chunk = K * LANES // steps
-    whole = pl.BlockSpec((LZ, ROWS, chunk), lambda i: (0, 0, i))
+    anywhere = pl.BlockSpec(memory_space=pl.ANY)
     return pl.pallas_call(
         natural,
-        grid=(steps,),
         out_shape=(shape, shape),
-        in_specs=[pl.BlockSpec((chunk, LANES), lambda i: (i, 0))],
-        out_specs=(whole, whole),
+        in_specs=[anywhere],
+        out_specs=(anywhere, anywhere),
+        scratch_shapes=[pltpu.VMEM((K * LANES, LANES), F32), pltpu.VMEM(source_heating.shape, F32), pltpu.VMEM(source_heating.shape, F32),
+                        pltpu.SemaphoreType.DMA((3, OUT_PARTS))],
     )(turned)
 
 

time: 70.1 us -> 65 us (0.927)
  Pallas kernels: 68.6 us -> 63.6 us
    pallas_call x1, Pallas kernels: 65 us -> 61.3 us  [local(): pl.pallas_call(functools.partial(kernel, n_tile), out_shape=jax.ShapeDtyp...]
    pallas_call x1, Pallas kernels: 3.56 us -> 2.28 us  [local(): pl.pallas_call(natural, out_shape=(shape, shape), in_specs=[anywhere], ou...]
where the time goes in v4:
time: 65 us; the launch traced here: 64.9 us
  Pallas kernels  63.6 us (98%)
  between operations  1.28 us (2%)
    pallas_call x1, Pallas kernels, local(): pl.pallas_call(functools.partial(kernel, n_tile), out_shape=jax.ShapeDtyp...  61.3 us
    pallas_call x1, Pallas kernels, local(): pl.pallas_call(natural, out_shape=(shape, shape), in_specs=[anywhere], ou...  2.28 us

profile of v4, /device:TPU:1, one launch (start us, length us, event | category | flops | bytes accessed | tf_op | source)
XLA Modules:
  0.0 64.9 jit_solution(4314711238935606328)
XLA Ops:
  1.3 61.3 %shard_map.68.turned_in = f32[2048,128]{1,0:T(8,128)} custom-call(f32[4,16,2048]{2,1,0:T(8,128)} %f_in.1, f32[6]{0:T(128)} %mats_in.1, s32[4]{0:T(128)} %material_in.1, f32[1]{0:T(128)S(6)} %copy.7.via_cond_in, s32[1,4,24]{2,1,0:T(4,128)} %bitcast.1), custom_call_target="tpu_custom_call" | custom-call | tf_op jit(solution)/shard_map/pallas_call | solution.py:654
  62.6 2.3 %shard_map.69 = (f32[4,16,2048]{2,1,0:T(8,128)}, f32[4,16,2048]{2,1,0:T(8,128)}) custom-call(f32[2048,128]{1,0:T(8,128)} %shard_map.68.turned_in), custom_call_target="tpu_custom_call" | custom-call | tf_op jit(solution)/shard_map/pallas_call | solution.py:678

commit v5 on v4

--- a/solution.py
+++ b/solution.py
@@ -22,6 +22,7 @@
 H2 = 6
 N2 = 1 + 2 * H2
 NZ = 16
+STRIP = 8
 
 
 def rows_of(y, count=1):
@@ -45,8 +46,21 @@
         fn(y)
 
 
+def strip_loop(lo, hi, unroll, fn):
+    whole = (hi - lo) // unroll
+
+    def body(i, carry):
+        fn(lo + i * unroll, unroll)
+        return carry
+
+    if whole:
+        lax.fori_loop(0, whole, body, 0)
+    if lo + whole * unroll < hi:
+        fn(lo + whole * unroll, hi - lo - whole * unroll)
+
+
 def kernel(n_tile, f_in, mats_in, material_in, via_cond_in, blocks_in, out, mats, material, via_cond, blocks, f_vm, f, v0, v1, v2, vn, vd_top, wlo, whi, pall, cz,
-           turn, restr, r1g, r1, w1, u1, l1, a1, b1, r2, w2, u2, l2, a2, b2, via1, pk, send_sem, recv_sem, in_sem):
+           turn, restr, r1g, r1, w1, u1, l1, a1, b1, r2, w2, u2, l2, a2, b2, via1, pk, ctab, send_sem, recv_sem, in_sem):
     d = lax.axis_index("die")
     t = lax.axis_index("tile")
 
@@ -84,7 +98,7 @@
         small[g].start()
 
     partners = [(1, 0), (2, 0), (3, 0), (1, 1), (1, -1), (-1, 1), (-1, -1)]
-    partners += [(0, s * j) for j in range(1, H2 + 1) for s in (1, -1)]
+    partners += [(0, s * j) for j in range(1, 5) for s in (1, -1)]
     barrier = pltpu.get_barrier_semaphore()
     for dd, dt in partners:
         pl.semaphore_signal(barrier, inc=1, device_id=at(dd, dt), device_id_type=pl.DeviceIdType.MESH)
@@ -146,7 +160,6 @@
         for k in range(K):
             vn[j, pl.ds(k, NYW, stride=K), :] = plane[0:NYW, k * LANES:(k + 1) * LANES]
 
-    via_plane(2)
     pl.semaphore_wait(barrier, len(partners))
 
     own = rows_of(HY, ROWS)
@@ -174,6 +187,7 @@
             v2[w, rows_of(y), :] = zero_row
 
     row_loop(0, NYW, 2, clear_v2)
+    via_plane(2)
     arrived(par)
     via_plane(1)
 
@@ -257,92 +271,91 @@
         via_plane(3)
         row_loop(0, NYW, 4, far_weights)
 
-    def beside(x):
-        nxt = pltpu.roll(x, K - 1, 0)
-        prv = pltpu.roll(x, 1, 0)
-        n_lo, n_hi = nxt[0:8], nxt[8:16]
-        p_lo, p_hi = prv[0:8], prv[8:16]
-        n_in = jnp.where(lanes8 == LANES - 1, 0.0, pltpu.roll(n_hi, LANES - 1, 1))
-        p_in = jnp.where(lanes8 == 0, 0.0, pltpu.roll(p_lo, 1, 1))
-        n_hi = jnp.where(subs8 == 7, n_in, n_hi)
-        p_lo = jnp.where(subs8 == 0, p_in, p_lo)
-        return jnp.concatenate([n_lo + p_lo, n_hi + p_hi], axis=0)
-
-    def flows(src, w, y, consts, above=True, below=True):
-        c, u, lo = consts
+    def beside(src, w, y):
+        base = y * K if isinstance(y, int) else pl.multiple_of(y * K, K)
+        first = jnp.broadcast_to(src[w, pl.ds(base, 1), :], (8, LANES))
+        final = jnp.broadcast_to(src[w, pl.ds(base + K - 1, 1), :], (8, LANES))
+        n_in = jnp.where(lanes8 == LANES - 1, 0.0, pltpu.roll(first, LANES - 1, 1))
+        p_in = jnp.where(lanes8 == 0, 0.0, pltpu.roll(final, 1, 1))
+        n_hi = jnp.where(subs8 == 7, n_in, src[w, pl.ds(base + 9, 8), :])
+        p_lo = jnp.where(subs8 == 0, p_in, src[w, pl.ds(base - 1, 8), :])
+        lo = src[w, pl.ds(base + 1, 8), :] + p_lo
+        return jnp.concatenate([lo, n_hi + src[w, pl.ds(base + 7, 8), :]], axis=0)
+
+    for w in range(NW):
+        c, u, lo = splat(w)
+        ctab[w, 0:1, :] = c
+        if u is not None:
+            ctab[w, 1:2, :] = u
+        if lo is not None:
+            ctab[w, 2:3, :] = lo
+        if u is not None and lo is not None:
+            ctab[w, 3:4, :] = OMEGA / (4.0 * c + u + lo)
+
+    def const(w, i):
+        return ctab[w, i:i + 1, :]
+
+    def flows(src, w, y, count, above=True, below=True):
         ty, m = w % LZ, w // LZ
-        x = src[w, rows_of(y), :]
-        side = (src[w, rows_of(y - 1), :] + src[w, rows_of(y + 1), :]) + beside(x)
-        total = f[w, rows_of(y), :] + c * side
-        if above:
-            total += (vn[m + 1, rows_of(y), :] if ty == 3 else u) * src[w + 1, rows_of(y), :]
-        if below:
-            total += (vn[m, rows_of(y), :] if ty == 0 else lo) * src[w - 1, rows_of(y), :]
-        return x, total
-
-    def plain_weight(consts):
-        c, u, lo = consts
-        return OMEGA / (4.0 * c + u + lo)
-
-    def weight(w, y, plain):
+        xs = [src[w, rows_of(y + j), :] for j in range(-1, count + 1)]
+        c = const(w, 0)
+        u = const(w, 1) if ty < 3 else None
+        lo = const(w, 2) if ty > 0 else None
+        out = []
+        for j in range(count):
+            side = (xs[j] + xs[j + 2]) + beside(src, w, y + j)
+            total = f[w, rows_of(y + j), :] + c * side
+            if above:
+                total += (vn[m + 1, rows_of(y + j), :] if ty == 3 else u) * src[w + 1, rows_of(y + j), :]
+            if below:
+                total += (vn[m, rows_of(y + j), :] if ty == 0 else lo) * src[w - 1, rows_of(y + j), :]
+            out.append((xs[j + 1], total))
+        return out
+
+    def weight(w, y):
         ty, m = w % LZ, w // LZ
         if ty == 0:
             return wlo[m, rows_of(y), :]
         if ty == 3:
             return whi[m, rows_of(y), :]
-        return plain * fine_valid(y)
-
-    def layer_consts(layers):
-        consts = {w: splat(w) for w in layers}
-        plain = {w: plain_weight(consts[w]) for w in layers if w % LZ in (1, 2)}
-        return consts, plain
+        return const(w, 3) * fine_valid(y)
 
     def start_from_zero(dst, layers, y_lo, y_hi):
-        _, plain = layer_consts(layers)
-
         def body(y):
             for w in layers:
-                dst[w, rows_of(y), :] = weight(w, y, plain.get(w)) * f[w, rows_of(y), :]
+                dst[w, rows_of(y), :] = weight(w, y) * f[w, rows_of(y), :]
 
         row_loop(y_lo, y_hi, max(1, 16 // len(layers)), body)
 
-    def unroll_of(layers, rows):
-        return max(u for u in (1, 2, 3, 4, 6) if rows % u == 0 and u * len(layers) <= 24)
-
     def sweep(src, dst, layers, y_lo, y_hi):
-        consts, plain = layer_consts(layers)
-
-        def body(y):
+        def body(y, count):
             for w in layers:
-                x, total = flows(src, w, y, consts[w])
-                dst[w, rows_of(y), :] = KEEP * x + weight(w, y, plain.get(w)) * total
-
-        row_loop(y_lo, y_hi, unroll_of(layers, y_hi - y_lo), body)
-
-    def diagonal(w, y, consts):
-        c, u, lo = consts
+                for j, (x, total) in enumerate(flows(src, w, y, count)):
+                    dst[w, rows_of(y + j), :] = KEEP * x + weight(w, y + j) * total
+
+        strip_loop(y_lo, y_hi, STRIP, body)
+
+    def diagonal(w, y):
+        c = const(w, 0)
         if w == LZ:
-            return 4.0 * c + u + vn[1, rows_of(y), :]
+            return 4.0 * c + const(w, 1) + vn[1, rows_of(y), :]
         if w == LZ + 3:
-            return 4.0 * c + lo + vd_top[rows_of(y), :]
-        return 4.0 * c + u + lo
+            return 4.0 * c + const(w, 2) + vd_top[rows_of(y), :]
+        return 4.0 * c + const(w, 1) + const(w, 2)
 
     own_layers = list(range(LZ, 2 * LZ))
 
     def restricted_residual(src, slot):
-        consts, _ = layer_consts(own_layers)
-
         def body(i, carry):
-            sums = [None] * 6
-            for q in range(4):
-                y = HY + i * 4 + q
-                parts = []
-                for w in own_layers:
-                    x, total = flows(src, w, y, consts[w], above=w < LZ + 3, below=w > LZ)
-                    parts.append(total - diagonal(w, y, consts[w]) * x)
-                parts.append(vn[1, rows_of(y), :] * src[LZ, rows_of(y), :])
-                parts.append(vn[2, rows_of(y), :] * src[LZ + 3, rows_of(y), :])
-                sums = [p if s is None else s + p for s, p in zip(sums, parts)]
+            y = HY + i * 4
+            sums = []
+            for w in own_layers:
+                rows = flows(src, w, y, 4, above=w < LZ + 3, below=w > LZ)
+                parts = [total - diagonal(w, y + q) * x for q, (x, total) in enumerate(rows)]
+                sums.append((parts[0] + parts[1]) + (parts[2] + parts[3]))
+            for j, w in ((1, LZ), (2, LZ + 3)):
+                parts = [vn[j, rows_of(y + q), :] * src[w, rows_of(y + q), :] for q in range(4)]
+                sums.append((parts[0] + parts[1]) + (parts[2] + parts[3]))
             for s in range(4):
                 restr[pl.ds(pl.multiple_of((i * 4 + s) * K, K), K), :] = sums[s]
             for s in range(2):
@@ -598,14 +611,12 @@
     sweep(v0, v1, deep[1:-1], HY - 2, HY + ROWS + 2)
     sweep(v1, v0, deep[2:-2], HY - 1, HY + ROWS + 1)
 
-    consts, _ = layer_consts(own_layers)
-
-    def defect(y):
+    def defect(y, count):
         for w in own_layers:
-            x, total = flows(v0, w, y, consts[w])
-            v2[w, rows_of(y), :] = total - diagonal(w, y, consts[w]) * x
-
-    row_loop(HY, HY + ROWS, 4, defect)
+            for j, (x, total) in enumerate(flows(v0, w, y, count)):
+                v2[w, rows_of(y + j), :] = total - diagonal(w, y + j) * x
+
+    strip_loop(HY, HY + ROWS, 4, defect)
 
     for k in range(K):
         block = jnp.concatenate([src[w, pl.ds(HY * K + k, ROWS, stride=K), :]
@@ -668,6 +679,7 @@
             tiles(N1 * 4), tiles(N1 * 4), tiles(N1 * 4), tiles(N1 * 4), tiles(N1 * 4),
             tiles(2, N2), tiles(N2), tiles(N2), tiles(N2), tiles(N2), tiles(N2),
             pltpu.VMEM((4, 80, LANES), F32), pltpu.VMEM((8, LANES), F32),
+            pltpu.VMEM((NW, 8, LANES), F32),
             pltpu.SemaphoreType.DMA((N_COPIES,)),
             pltpu.SemaphoreType.DMA((N_COPIES,)),
             pltpu.SemaphoreType.DMA((8,)),

time: 65 us -> 62.4 us (0.960)
  Pallas kernels: 63.6 us -> 61 us
    pallas_call x1, Pallas kernels: 61.3 us -> 58.7 us  [local(): pl.pallas_call(functools.partial(kernel, n_tile), out_shape=jax.ShapeDtyp...]
where the time goes in v5:
time: 62.4 us; the launch traced here: 62.3 us
  Pallas kernels  61 us (98%)
  between operations  1.28 us (2%)
    pallas_call x1, Pallas kernels, local(): pl.pallas_call(functools.partial(kernel, n_tile), out_shape=jax.ShapeDtyp...  58.7 us
    pallas_call x1, Pallas kernels, local(): pl.pallas_call(natural, out_shape=(shape, shape), in_specs=[anywhere], ou...  2.28 us

profile of v5, /device:TPU:1, one launch (start us, length us, event | category | flops | bytes accessed | tf_op | source)
XLA Modules:
  0.0 62.3 jit_solution(17219129752585993772)
XLA Ops:
  1.3 58.7 %shard_map.68.turned_in = f32[2048,128]{1,0:T(8,128)} custom-call(f32[4,16,2048]{2,1,0:T(8,128)} %f_in.1, f32[6]{0:T(128)} %mats_in.1, s32[4]{0:T(128)} %material_in.1, f32[1]{0:T(128)S(6)} %copy.7.via_cond_in, s32[1,4,24]{2,1,0:T(4,128)} %bitcast.1), custom_call_target="tpu_custom_call" | custom-call | tf_op jit(solution)/shard_map/pallas_call | solution.py:665
  60.0 2.3 %shard_map.69 = (f32[4,16,2048]{2,1,0:T(8,128)}, f32[4,16,2048]{2,1,0:T(8,128)}) custom-call(f32[2048,128]{1,0:T(8,128)} %shard_map.68.turned_in), custom_call_target="tpu_custom_call" | custom-call | tf_op jit(solution)/shard_map/pallas_call | solution.py:690

commit v6 on v5

--- a/solution.py
+++ b/solution.py
@@ -22,7 +22,7 @@
 H2 = 6
 N2 = 1 + 2 * H2
 NZ = 16
-STRIP = 8
+STRIP = 12
 
 
 def rows_of(y, count=1):

time: 62.4 us -> 61.3 us (0.982)
  Pallas kernels: 61 us -> 59.9 us
    pallas_call x1, Pallas kernels: 58.7 us -> 57.6 us  [local(): pl.pallas_call(functools.partial(kernel, n_tile), out_shape=jax.ShapeDtyp...]
where the time goes in v6:
time: 61.3 us; the launch traced here: 61.2 us
  Pallas kernels  59.9 us (98%)
  between operations  1.28 us (2%)
    pallas_call x1, Pallas kernels, local(): pl.pallas_call(functools.partial(kernel, n_tile), out_shape=jax.ShapeDtyp...  57.6 us
    pallas_call x1, Pallas kernels, local(): pl.pallas_call(natural, out_shape=(shape, shape), in_specs=[anywhere], ou...  2.28 us

profile of v6, /device:TPU:1, one launch (start us, length us, event | category | flops | bytes accessed | tf_op | source)
XLA Modules:
  0.0 61.2 jit_solution(13961465100362392601)
XLA Ops:
  1.3 57.6 %shard_map.68.turned_in = f32[2048,128]{1,0:T(8,128)} custom-call(f32[4,16,2048]{2,1,0:T(8,128)} %f_in.1, f32[6]{0:T(128)} %mats_in.1, s32[4]{0:T(128)} %material_in.1, f32[1]{0:T(128)S(6)} %copy.7.via_cond_in, s32[1,4,24]{2,1,0:T(4,128)} %bitcast.1), custom_call_target="tpu_custom_call" | custom-call | tf_op jit(solution)/shard_map/pallas_call | solution.py:665
  58.9 2.3 %shard_map.69 = (f32[4,16,2048]{2,1,0:T(8,128)}, f32[4,16,2048]{2,1,0:T(8,128)}) custom-call(f32[2048,128]{1,0:T(8,128)} %shard_map.68.turned_in), custom_call_target="tpu_custom_call" | custom-call | tf_op jit(solution)/shard_map/pallas_call | solution.py:690
